TPU v7x, 32 devices: a whole 2x2x4 slice. The times are simulated.
32 devices in a mesh: grp: 8 (over z, x), sub: 4 (over y, core).
Axes of the slice: x: 2, y: 2, z: 4, core: 2. Of those that a mesh axis runs over, the one named last changes fastest.
Arguments:
- residual: float32 [98304], P(('grp', 'sub')), may hold values from -6 to 6
- edge_scale: float32 [98304], P(('grp', 'sub')), may hold values from 0.2 to 1
- tangent: float32 [3, 98304], P(None, ('grp', 'sub')), may hold values from -6 to 6
- edge_tail: int32 [98304], P(('grp', 'sub')), may hold values from 0 to 511
- edge_head: int32 [98304], P(('grp', 'sub')), may hold values from 0 to 4607
- stencil_index: int32 [14, 16384], P(None, ('grp', 'sub')), may hold values from 0 to 4607
- stencil_coef: bfloat16 [4, 14, 16384], P(None, None, ('grp', 'sub')), may hold values from -1 to -0.099609375
- diag_margin: float32 [4, 16384], P(None, ('grp', 'sub')), may hold values from 0.05 to 0.5
- send_index: int32 [16, 8, 512], P('grp', 'sub'), may hold values from 0 to 511
Outputs:
- correction: float32 [98304], P(('grp', 'sub'))
Inputs may be any that keep to these rules, and one draw needn't show every extreme that they name: `edge_tail`: positions among a device's own nodes. `edge_head`: positions in the device's extended list: own nodes first, then the 8 received blocks. `stencil_index`: positions in the extended list of the device that holds the row. `send_index`: positions among the device's own nodes; an entry may repeat.
All inputs are finite; a program needn't handle non-finite values.
Results may differ from a plain program's by a relative error of at most 0.0003.
Values sent between devices are 32-bit elements; how exact they have to be, the bound alone decides.
A program may use at most 64 MiB of HBM per device.

v0:
```python
import functools

import jax
import jax.numpy as jnp
from jax import lax
from jax.experimental import pallas as pl
from jax.experimental.pallas import tpu as pltpu
from jax.sharding import PartitionSpec as P

SWEEPS = 4
LANES = 128
OPP = (0, 2, 1, 4, 3)
MESH = pl.DeviceIdType.MESH
DNUMS = lax.GatherDimensionNumbers(
    offset_dims=(),
    collapsed_slice_dims=(1,),
    start_index_map=(1,),
    operand_batching_dims=(0,),
    start_indices_batching_dims=(0,),
)
F32 = jnp.float32
BF16 = jnp.bfloat16


def lane_gather(table, lane):
    return lax.gather(
        table,
        lane[..., None],
        DNUMS,
        slice_sizes=(1, 1),
        mode=lax.GatherScatterMode.PROMISE_IN_BOUNDS,
    )


def nt_dot(a, b):
    return lax.dot_general(a, b, (((1,), (1,)), ((), ())), preferred_element_type=F32)


def kernel(
    res_h, tan_h, tail_h, head_h, sidx_h, coef_h, marg_h, send_h,
    out_ref,
    res, tan, tail, head, sidx, coef, marg, own_send,
    got_send, psend, got_p, tab, onehot, spread, onehot2, spread2, onehot3, spread3, tsum,
    cf, bsc, diag, hq, hl, sq, sl, tan2,
    local_sem, send_sem, recv_sem,
):
    G, S = lax.axis_size("grp"), lax.axis_size("sub")
    g, s = lax.axis_index("grp"), lax.axis_index("sub")
    gm, gp = lax.rem(g + G - 1, G), lax.rem(g + 1, G)
    sm, sp = lax.rem(s + S - 1, S), lax.rem(s + 1, S)
    peer = (None, (gm, s), (gp, s), (g, sm), (g, sp))
    order = (4, 3, 2, 1)
    nrow = marg.shape[1] // LANES
    erow = res.shape[0]
    stencil = sidx.shape[0]
    vrow = 4 * nrow
    nq = 5 * nrow
    hrow = got_send.shape[3] // LANES

    barrier = pltpu.get_barrier_semaphore()
    for o in order:
        pl.semaphore_signal(barrier, inc=1, device_id=peer[o], device_id_type=MESH)
    pairs = (
        (tail_h, tail), (res_h, res), (tan_h, tan), (head_h, head),
        (send_h, own_send), (coef_h, coef), (marg_h, marg), (sidx_h, sidx),
    )
    local = [
        pltpu.make_async_copy(src, dst, local_sem.at[i]) for i, (src, dst) in enumerate(pairs)
    ]
    for c in local:
        c.start()

    def exchange(rnd, src, dst):
        copies = {}
        for o in order:
            copies[o] = pltpu.make_async_remote_copy(
                src_ref=src(o),
                dst_ref=dst(OPP[o]),
                send_sem=send_sem.at[rnd, o - 1],
                recv_sem=recv_sem.at[rnd, OPP[o] - 1],
                device_id=peer[o],
                device_id_type=MESH,
            )
            copies[o].start()
        return copies

    def arrived(copies, o):
        copies[OPP[o]].wait_recv()

    near = 2 - lax.rem(g, 2)
    walk = (4, 3, near, 3 - near)

    def table_here(rnd, o):
        pltpu.make_async_remote_copy(
            src_ref=tab.at[rnd, pl.ds(0, vrow)],
            dst_ref=tab.at[rnd, pl.ds(o * vrow, vrow)],
            send_sem=send_sem.at[2 + rnd, 0],
            recv_sem=recv_sem.at[2 + rnd, o - 1],
            device_id=peer[4],
            device_id_type=MESH,
        ).wait_recv()

    for c in local:
        c.wait()
    riota = lax.broadcasted_iota(jnp.int32, (vrow, LANES), 0)
    kind = riota // nrow
    rpart = riota - kind * nrow
    liota = lax.broadcasted_iota(jnp.int32, (LANES, LANES), 0)

    def terms(t, sign):
        r = res[t : t + 1, :]
        first = jnp.broadcast_to(r if sign > 0 else -r, (vrow, LANES))
        half = 0.5 * r
        val = first
        for c in range(3):
            v = tan[c : c + 1, t * LANES : (t + 1) * LANES] * half
            val = jnp.where(kind == c + 1, v, val)
        hi = val.astype(BF16).astype(F32)
        return hi, val - hi

    def scatter(spread_ref, onehot_ref, lanes_of, rows_of, owners, sign):
        for t in range(erow):
            cols = slice(t * LANES, (t + 1) * LANES)
            onehot_ref[:, cols] = jnp.where(liota == lanes_of(t), 1.0, 0.0).astype(BF16)
            hi, lo = terms(t, sign)
            row = rows_of(t)
            for o in range(owners):
                hit = row == rpart + o * nrow
                for p, v in enumerate((hi, lo)):
                    base = (p * owners + o) * vrow
                    spread_ref[base : base + vrow, cols] = jnp.where(hit, v, 0.0).astype(BF16)
        both = nt_dot(spread_ref[...], onehot_ref[...])
        return both[: owners * vrow] + both[owners * vrow :]

    own_sum = scatter(
        spread, onehot,
        lambda t: tail[t : t + 1, :] & (LANES - 1),
        lambda t: tail[t : t + 1, :] >> 7,
        1, -1,
    )

    parts = scatter(
        spread2, onehot2,
        lambda t: head[t : t + 1, :] & (LANES - 1),
        lambda t: head[t : t + 1, :] >> 7,
        (nrow + 8 * hrow) // nrow, 1,
    )
    psend[...] = parts[vrow:]
    own_sum = own_sum + parts[:vrow]
    sent = 2 * 4 * hrow

    lists = tuple((a, b, r) for a in range(2) for b in range(2) for r in range(hrow))

    def own_list(a, b, r):
        return own_send[a, b : b + 1, r * LANES : (r + 1) * LANES]

    for n, abr in enumerate(lists):
        hit = liota == (own_list(*abr) & (LANES - 1))
        onehot3[:, n * LANES : (n + 1) * LANES] = jnp.where(hit, 1.0, 0.0).astype(BF16)

    cf[...] = jnp.zeros_like(cf)
    for k in range(4):
        for r in range(nrow):
            cols = slice(r * LANES, (r + 1) * LANES)
            c = coef[:, k, cols].astype(F32)
            d = (1.0 + marg[k : k + 1, cols]) * jnp.sum(jnp.abs(c), axis=0, keepdims=True)
            inv = 1.0 / d
            diag[k * nrow + r : k * nrow + r + 1, :] = inv
            cf[k, :stencil, cols] = c * inv
    for c in range(3):
        for t in range(erow):
            tan2[c * erow + t : c * erow + t + 1, :] = tan[c : c + 1, t * LANES : (t + 1) * LANES]
    sq[...] = jnp.zeros_like(sq)
    sq[:stencil, :] = sidx[...]

    pl.semaphore_wait(barrier, 4)
    rounds = [
        exchange(
            1,
            lambda o: psend.at[pl.ds((o - 1) * sent, sent)],
            lambda o: got_p.at[pl.ds((o - 1) * sent, sent)],
        )
    ]
    rounds.append(exchange(0, lambda o: own_send, lambda o: got_send.at[o - 1]))

    for o in order:
        arrived(rounds[0], o)
    block = 4 * hrow
    for a in range(2):
        for b in range(2):
            first = a * sent + b * block
            second = (2 + b) * sent + a * block
            at = (a * 2 + b) * block
            tsum[at : at + block, :] = got_p[first : first + block, :] + got_p[second : second + block, :]
    for n, (a, b, r) in enumerate(lists):
        base = (a * 2 + b) * block + r
        val = jnp.broadcast_to(tsum[base : base + 1, :], (vrow, LANES))
        for k in range(1, 4):
            at = base + k * hrow
            val = jnp.where(kind == k, tsum[at : at + 1, :], val)
        hit = (own_list(a, b, r) >> 7) == rpart
        val = jnp.where(hit, val, 0.0)
        hi = val.astype(BF16)
        cols = slice(n * LANES, (n + 1) * LANES)
        spread3[:vrow, cols] = hi
        spread3[vrow:, cols] = (val - hi.astype(F32)).astype(BF16)
    back = nt_dot(spread3[...], onehot3[...])
    own_sum = own_sum + (back[:vrow] + back[vrow:])
    bsc[...] = own_sum * diag[...]

    halves = (
        None,
        ((1, 0), (1, 1)),
        ((0, 0), (0, 1)),
        ((0, 1), (1, 1)),
        ((0, 0), (1, 0)),
    )

    def compose(x):
        lane = x & (LANES - 1)
        row = x >> 7
        y = x
        at = nrow
        for o in range(1, 5):
            for a, b in halves[o]:
                for r in range(hrow):
                    line = got_send[o - 1, a, b : b + 1, r * LANES : (r + 1) * LANES]
                    line = jnp.broadcast_to(line + o * nrow * LANES, x.shape)
                    y = jnp.where(row == at, lane_gather(line, lane), y)
                    at += 1
        return y

    def compose_all():
        for o in order:
            arrived(rounds[1], o)
        for i in range(srows):
            for r in range(nrow):
                cols = slice(r * LANES, (r + 1) * LANES)
                y = compose(sq[i * 8 : i * 8 + 8, cols])
                sq[i * 8 : i * 8 + 8, cols] = y >> 7
                sl[i * 8 : i * 8 + 8, cols] = y & (LANES - 1)

    def compose_heads():
        for i in range(erow // 8):
            y = compose(head[i * 8 : i * 8 + 8, :])
            hq[i * 8 : i * 8 + 8, :] = y >> 7
            hl[i * 8 : i * 8 + 8, :] = y & (LANES - 1)

    srows = sq.shape[0] // 8

    def look(rnd, o, r, k, shape):
        at = o * vrow + k * nrow + r
        return jnp.broadcast_to(tab[rnd, pl.ds(at, 1), :], shape)

    def add_rows(rnd, o, rows, lanes, accs):
        for r in range(nrow):
            for i in range(len(rows)):
                hit = rows[i] == o * nrow + r
                for k in range(4):
                    v = lane_gather(look(rnd, o, r, k, rows[i].shape), lanes[i])
                    accs[i][k] = v if accs[i][k] is None else jnp.where(hit, v, accs[i][k])

    sub8 = lax.broadcasted_iota(jnp.int32, (8, LANES), 0)

    def fold(vecs):
        step = len(vecs) // 2
        while step:
            keep = (sub8 & step) == 0
            vecs = [
                jnp.where(keep, x, y) + pltpu.roll(jnp.where(keep, y, x), step, axis=0)
                if step == 4 else
                jnp.where(keep, x + pltpu.roll(x, 8 - step, axis=0), y + pltpu.roll(y, step, axis=0))
                for x, y in zip(vecs[:step], vecs[step:])
            ]
            step //= 2
        return vecs[0]

    for rnd in range(SWEEPS):
        if rnd == 0:
            tab[rnd, :vrow, :] = bsc[...]
        copies = exchange(
            2 + rnd,
            lambda o: tab.at[rnd, pl.ds(0, vrow)],
            lambda o: tab.at[rnd, pl.ds(o * vrow, vrow)],
        )
        rounds.append(copies)
        if rnd == 0:
            compose_all()
        if rnd == 1:
            compose_heads()
        if rnd < SWEEPS - 1:
            where = [(slice(i * 8, i * 8 + 8), slice(r * LANES, (r + 1) * LANES)) for i in range(srows) for r in range(nrow)]
            rows = [sq[w] for w in where]
            lanes = [sl[w] for w in where]
            accs = [[None] * 4 for _ in where]
            add_rows(rnd, 0, rows, lanes, accs)
            for o in walk:
                table_here(rnd, o)
                add_rows(rnd, o, rows, lanes, accs)
            totals = []
            for k in range(4):
                for r in range(nrow):
                    total = None
                    for i in range(srows):
                        n = i * nrow + r
                        v = accs[n][k] * cf[(k,) + where[n]]
                        total = v if total is None else total + v
                    totals.append(total)
            for at in range(0, vrow, 8):
                tab[rnd + 1, at : at + 8, :] = bsc[at : at + 8, :] - fold(totals[at : at + 8])

    last = SWEEPS - 1
    n3 = erow // 8
    where = [slice(i * 8, i * 8 + 8) for i in range(n3)]
    tails = [tail[w, :] for w in where]
    tacc = [[None] * 4 for _ in where]
    add_rows(last, 0, [t >> 7 for t in tails], [t & (LANES - 1) for t in tails], tacc)
    rows = [hq[w, :] for w in where]
    lanes = [hl[w, :] for w in where]
    hacc = [[None] * 4 for _ in where]
    add_rows(last, 0, rows, lanes, hacc)
    for o in walk:
        table_here(last, o)
        add_rows(last, o, rows, lanes, hacc)
    for i, w in enumerate(where):
        mixed = None
        for c in range(3):
            v = tan2[c * erow + i * 8 : c * erow + i * 8 + 8, :] * (tacc[i][c + 1] + hacc[i][c + 1])
            mixed = v if mixed is None else mixed + v
        out_ref[w, :] = (hacc[i][0] - tacc[i][0]) + 0.5 * mixed

    for copies in rounds:
        for o in order:
            copies[o].wait_send()


def body(
    residual, edge_scale, tangent, edge_tail, edge_head,
    stencil_index, stencil_coef, diag_margin, send_index,
):
    edges = residual.shape[0]
    erow = edges // LANES
    nodes = diag_margin.shape[1]
    nrow = nodes // LANES
    vrow = 4 * nrow
    stencil = stencil_index.shape[0]
    spad = -(-stencil // 8) * 8
    hrow = send_index.shape[2] // LANES
    blocks = (nrow + 8 * hrow) // nrow
    coef = jnp.transpose(stencil_coef, (1, 0, 2))
    square = lambda x: x.reshape(erow, LANES)
    anyspace = pl.BlockSpec(memory_space=pl.ANY)
    vm = pltpu.VMEM
    i32 = jnp.int32
    gathered = pl.pallas_call(
        kernel,
        out_shape=jax.ShapeDtypeStruct((erow, LANES), F32),
        in_specs=[anyspace] * 8,
        out_specs=pl.BlockSpec(memory_space=vm),
        scratch_shapes=[
            vm((erow, LANES), F32),
            vm(tangent.shape, F32),
            vm((erow, LANES), i32),
            vm((erow, LANES), i32),
            vm(stencil_index.shape, i32),
            vm(coef.shape, BF16),
            vm(diag_margin.shape, F32),
            vm(send_index.shape, i32),
            vm((4,) + send_index.shape, i32),
            vm((32 * hrow, LANES), F32),
            vm((32 * hrow, LANES), F32),
            vm((SWEEPS, 5 * vrow, LANES), F32),
            vm((LANES, edges), BF16),
            vm((2 * vrow, edges), BF16),
            vm((LANES, edges), BF16),
            vm((2 * blocks * vrow, edges), BF16),
            vm((LANES, 4 * send_index.shape[2]), BF16),
            vm((2 * vrow, 4 * send_index.shape[2]), BF16),
            vm((16 * hrow, LANES), F32),
            vm((4, spad, nodes), F32),
            vm((vrow, LANES), F32),
            vm((vrow, LANES), F32),
            vm((erow, LANES), i32),
            vm((erow, LANES), i32),
            vm((spad, nodes), i32),
            vm((spad, nodes), i32),
            vm((3 * erow, LANES), F32),
            pltpu.SemaphoreType.DMA((8,)),
            pltpu.SemaphoreType.DMA((SWEEPS + 2, 4)),
            pltpu.SemaphoreType.DMA((SWEEPS + 2, 4)),
        ],
        compiler_params=pltpu.CompilerParams(collective_id=0, has_side_effects=True),
    )(
        square(residual), tangent, square(edge_tail), square(edge_head),
        stencil_index, coef, diag_margin, send_index,
    )
    return edge_scale * residual + gathered.reshape(edges)


def solution(mesh):
    return jax.shard_map(
        body,
        mesh=mesh,
        in_specs=(
            P(("grp", "sub")),
            P(("grp", "sub")),
            P(None, ("grp", "sub")),
            P(("grp", "sub")),
            P(("grp", "sub")),
            P(None, ("grp", "sub")),
            P(None, None, ("grp", "sub")),
            P(None, ("grp", "sub")),
            P("grp", "sub", None),
        ),
        out_specs=P(("grp", "sub")),
        check_vma=False,
    )
```

profile of v0, /device:TPU:0, one launch (start us, length us, event | category | flops | bytes accessed | tf_op | source)
XLA Modules:
  0.0 30.7 jit_solution(6354892567285792682)
XLA Ops:
  0.0 0.0 copy-start
  0.0 0.0 copy-start.1
  0.0 29.4 %shard_map.91 = f32[24,128]{1,0:T(8,128)} custom-call(f32[24,128]{1,0:T(8,128)} %bitcast.7, f32[3,3072]{1,0:T(4,128)} %tan_h.1, s32[24,128]{1,0:T(8,128)} %bitcast.8, s32[24,128]{1,0:T(8,128)} %bitcast.9, s32[14,512]{1,0:T(8,128)} %sidx_h.1, bf16[14,4,512]{2,1,0:T(4,128)(2,1)} %bitcast.6, f32[4,512]{1,0:T(4,128)} %marg_h.1, s32[2,2,512]{2,1,0:T(2,128)} %send_h.1), custom_call_target="tpu_custom_call" | custom-call | tf_op jit(solution)/shard_map/pallas_call | solution.py:355
  29.4 0.0 copy-done
  29.4 0.0 copy-done.1
  29.4 1.3 %bitcast_add_fusion = f32[3072]{0:T(1024)} fusion(f32[24,128]{1,0:T(8,128)} %shard_map.91, f32[3072]{0:T(1024)S(1)} %copy-done.1, f32[3072]{0:T(1024)S(1)} %copy-done), kind=kLoop, calls=%fused_computation | loop fusion | flops 6144 | bytes 49152 | tf_op jit(solution)/shard_map/add | solution.py:397
Async XLA Ops:
  0.0 29.4 %copy-start = (f32[3072]{0:T(1024)S(1)}, f32[3072]{0:T(1024)}, u32[]{:S(2)}) copy-start(f32[3072]{0:T(1024)} %param.9) | copy-start | bytes 36868
  0.0 29.4 %copy-start.1 = (f32[3072]{0:T(1024)S(1)}, f32[3072]{0:T(1024)}, u32[]{:S(2)}) copy-start(f32[3072]{0:T(1024)} %param.10) | copy-start | bytes 36868
where the time goes:
time: 30.9 us; the launch traced here: 30.7 us
  Pallas kernels  29.4 us (95%)
  other arithmetic  1.31 us (4%)
    pallas_call x1, Pallas kernels, body(): pl.pallas_call(kernel, out_shape=jax.ShapeDtypeStruct((erow, LANES), F32)...  29.4 us
    add x1, other arithmetic, body(): return edge_scale * residual + gathered.reshape(edges)  1.31 us

commit v1 on v0

v1 whole, which is shorter than its diff:
```python
import jax
import jax.numpy as jnp
from jax import lax
from jax.experimental import pallas as pl
from jax.experimental.pallas import tpu as pltpu
from jax.sharding import PartitionSpec as P

SWEEPS = 4
LANES = 128
SLOTS = 8
MESH = pl.DeviceIdType.MESH
DNUMS = lax.GatherDimensionNumbers(
    offset_dims=(),
    collapsed_slice_dims=(1,),
    start_index_map=(1,),
    operand_batching_dims=(0,),
    start_indices_batching_dims=(0,),
)
F32 = jnp.float32
BF16 = jnp.bfloat16
I32 = jnp.int32

OWN, FAR, NEAR, SM, SP = range(5)
FAR_NEAR, FAR_SM, FAR_SP = 5, 6, 7
GHOST_SLOT = (FAR, OWN, FAR_NEAR, FAR_SM, FAR_SP)


def lane_gather(table, lane):
    return lax.gather(
        table,
        lane[..., None],
        DNUMS,
        slice_sizes=(1, 1),
        mode=lax.GatherScatterMode.PROMISE_IN_BOUNDS,
    )


def nt_dot(a, b):
    return lax.dot_general(a, b, (((1,), (1,)), ((), ())), preferred_element_type=F32)


def kernel(
    res_h, tan_h, tail_h, head_h, sidx_h, coef_h, marg_h, send_h, scale_h,
    out_ref,
    res, tan, tail, head, sidx, coef, marg, own_send, scale,
    got_send, psend, got_p, tab, onehot, spread_o, spread_f, spread_r, onehot3, spread3, tsum,
    cf, gcf, bsc, diag, hq, hl, sq, gq, tan2,
    local_sem, send_sem, recv_sem, tab_send, tab_recv, ghost_send, ghost_recv,
):
    G, S = lax.axis_size("grp"), lax.axis_size("sub")
    g, s = lax.axis_index("grp"), lax.axis_index("sub")
    odd = lax.rem(g, 2)
    even = 1 - odd
    gf, gn = lax.rem(g + G - 1 + 2 * odd, G), lax.rem(g + 1 + (G - 2) * odd, G)
    sm, sp = lax.rem(s + S - 1, S), lax.rem(s + 1, S)
    peer = {FAR: (gf, s), NEAR: (gn, s), SM: (g, sm), SP: (g, sp)}
    nn_to = (lax.rem(g + 2 + (G - 4) * odd, G), s)
    nn_from = (lax.rem(g + G - 2 + 4 * odd, G), s)
    greeted = [peer[FAR], peer[NEAR], peer[SM], peer[SP], nn_to, nn_from, (gf, sm), (gf, sp)]
    back = {FAR: FAR, NEAR: NEAR, SM: SP, SP: SM}
    nrow = marg.shape[1] // LANES
    erow = res.shape[0]
    stencil = sidx.shape[0]
    vrow = 4 * nrow
    sent = 2 * vrow
    srows = sq.shape[0] // 8

    barrier = pltpu.get_barrier_semaphore()
    for who in greeted:
        pl.semaphore_signal(barrier, inc=1, device_id=who, device_id_type=MESH)
    pairs = (
        (head_h, head), (res_h, res), (tan_h, tan), (send_h, own_send), (tail_h, tail),
        (coef_h, coef), (marg_h, marg), (sidx_h, sidx), (scale_h, scale),
    )
    local = [
        pltpu.make_async_copy(src, dst, local_sem.at[i]) for i, (src, dst) in enumerate(pairs)
    ]
    for c in local:
        c.start()

    started = []

    def remote(src, dst, ssem, rsem, who):
        copy = pltpu.make_async_remote_copy(
            src_ref=src, dst_ref=dst, send_sem=ssem, recv_sem=rsem, device_id=who, device_id_type=MESH,
        )
        copy.start()
        started.append(copy)

    def landed(dst, rsem):
        pltpu.make_async_remote_copy(
            src_ref=dst, dst_ref=dst, send_sem=rsem, recv_sem=rsem, device_id=peer[SP], device_id_type=MESH,
        ).wait_recv()

    def part_rows(ref, o):
        return ref.at[pl.ds((o - 1) * sent, sent)]

    def send_part(o):
        remote(part_rows(psend, o), part_rows(got_p, back[o]), send_sem.at[0, o - 1], recv_sem.at[0, back[o] - 1], peer[o])

    def send_list(o):
        remote(own_send, got_send.at[back[o] - 1], send_sem.at[1, o - 1], recv_sem.at[1, back[o] - 1], peer[o])

    def slot_rows(rnd, slot):
        return tab.at[rnd, pl.ds(slot * vrow, vrow)]

    def send_table(rnd, who, slot):
        remote(slot_rows(rnd, OWN), slot_rows(rnd, slot), tab_send.at[rnd, slot - 1], tab_recv.at[rnd, slot - 1], who)

    def table_here(rnd, slot):
        landed(slot_rows(rnd, slot), tab_recv.at[rnd, slot - 1])

    riota = lax.broadcasted_iota(I32, (vrow, LANES), 0)
    kind = riota // nrow
    rpart = (riota - kind * nrow).astype(F32).astype(BF16)
    lane16 = lax.broadcasted_iota(I32, (16, LANES), 0).astype(F32).astype(BF16)
    one, zero = jnp.ones((), BF16), jnp.zeros((), BF16)

    def cols_of(t):
        return slice(t * LANES, (t + 1) * LANES)

    def wide(row, rows):
        return jnp.broadcast_to(row.astype(F32), (rows, LANES)).astype(BF16)

    def lanes_onehot(ref, cols, x):
        lane = wide(x & (LANES - 1), 16)
        for q in range(LANES // 16):
            mine = lane16 + jnp.full((), 16 * q, BF16)
            ref[q * 16 : q * 16 + 16, cols] = jnp.where(mine == lane, one, zero)

    def split(val):
        hi = val.astype(BF16)
        return hi, (val - hi.astype(F32)).astype(BF16)

    def terms(t, sign):
        r = res[t : t + 1, :]
        val = jnp.broadcast_to(r if sign > 0 else -r, (vrow, LANES))
        half = 0.5 * r
        for c in range(3):
            val = jnp.where(kind == c + 1, tan[c : c + 1, cols_of(t)] * half, val)
        return split(val)

    def scatter(ref, rows_of, bases, sign, make=None):
        n = len(bases)
        for t in range(erow):
            cols = cols_of(t)
            x = rows_of[t : t + 1, :]
            if make:
                lanes_onehot(onehot, cols, x)
            pieces = terms(t, sign)
            row = wide(x >> 7, vrow)
            for j, base in enumerate(bases):
                hit = row == rpart + base
                for p, v in enumerate(pieces):
                    at = (p * n + j) * vrow
                    ref[at : at + vrow, cols] = jnp.where(hit, v, zero)
        both = nt_dot(ref[...], onehot[...])
        return both[: n * vrow] + both[n * vrow :]

    def base_of(block):
        return (jnp.asarray(block, I32) * nrow).astype(F32).astype(BF16)

    far_block, near_block = 1 + 2 * odd, 3 - 2 * odd

    for c in local[:3]:
        c.wait()
    psend[0:sent] = scatter(spread_f, head, [base_of(far_block), base_of(far_block + 1)], 1, make=True)
    pl.semaphore_wait(barrier, len(greeted))
    send_part(FAR)
    rest = scatter(
        spread_r, head,
        [base_of(b) for b in (near_block, near_block + 1, 5, 6, 7, 8, 0)], 1,
    )
    psend[sent:] = rest[: 3 * sent]
    own_sum = rest[3 * sent :]
    for o in (NEAR, SM, SP):
        send_part(o)
    local[3].wait()
    for o in (FAR, NEAR, SM, SP):
        send_list(o)
    for c in local[4:]:
        c.wait()

    cf[...] = jnp.zeros_like(cf)
    for k in range(4):
        for r in range(nrow):
            cols = cols_of(r)
            c = coef[:, k, cols].astype(F32)
            d = (1.0 + marg[k : k + 1, cols]) * jnp.sum(jnp.abs(c), axis=0, keepdims=True)
            inv = 1.0 / d
            diag[k * nrow + r : k * nrow + r + 1, :] = inv
            cf[k, :stencil, cols] = c * inv
    remote(cf, gcf, ghost_send.at[0], ghost_recv.at[0], peer[FAR])

    for t in range(erow):
        lanes_onehot(onehot, cols_of(t), tail[t : t + 1, :])
    own_sum = own_sum + scatter(spread_o, tail, [base_of(0)], -1)

    a_of = (odd, even)
    lists = tuple((f, b, r) for f in range(2) for b in range(2) for r in range(nrow))

    def own_list(f, b, r):
        return own_send[a_of[f], b : b + 1, cols_of(r)]

    for n, fbr in enumerate(lists):
        lanes_onehot(onehot3, cols_of(n), own_list(*fbr))
    for c in range(3):
        for t in range(erow):
            tan2[c * erow + t : c * erow + t + 1, :] = tan[c : c + 1, cols_of(t)]
    sq[...] = jnp.zeros_like(sq)
    sq[:stencil, :] = sidx[...]

    def place(ref, at, f, b, r):
        hit = wide(own_list(f, b, r) >> 7, vrow) == rpart
        base = b * vrow + r + at
        val = jnp.broadcast_to(ref[base : base + 1, :], (vrow, LANES))
        for k in range(1, 4):
            row = base + k * nrow
            val = jnp.where(kind == k, ref[row : row + 1, :], val)
        return [jnp.where(hit, v, zero) for v in split(val)]

    for o in (SP, SM, NEAR):
        landed(part_rows(got_p, o), recv_sem.at[0, o - 1])
    for f in range(2):
        for b in range(2):
            first = pl.multiple_of((2 + b) * sent + a_of[f] * vrow, vrow)
            val = got_p[pl.ds(first, vrow), :]
            if f:
                val = val + got_p[sent + b * vrow : sent + (b + 1) * vrow, :]
            at = (f * 2 + b) * vrow
            tsum[at : at + vrow, :] = val
    for n, (f, b, r) in enumerate(lists):
        for p, v in enumerate(place(tsum, f * sent, f, b, r)):
            spread3[p * vrow : (p + 1) * vrow, cols_of(n)] = v
    got = nt_dot(spread3[...], onehot3[...])
    own_sum = own_sum + (got[:vrow] + got[vrow:])

    landed(part_rows(got_p, FAR), recv_sem.at[0, FAR - 1])
    half = len(lists) // 2
    for n, (f, b, r) in enumerate(lists[:half]):
        for p, v in enumerate(place(got_p, 0, f, b, r)):
            spread3[p * vrow : (p + 1) * vrow, cols_of(n)] = v
    got = nt_dot(spread3[:, : half * LANES], onehot3[:, : half * LANES])
    bsc[...] = (own_sum + (got[:vrow] + got[vrow:])) * diag[...]
    tab[0, :vrow, :] = bsc[...]

    def send_round(rnd, deep):
        if deep:
            send_table(rnd, peer[FAR], FAR)
            send_table(rnd, (gf, sp), FAR_SM)
            send_table(rnd, (gf, sm), FAR_SP)
            send_table(rnd, nn_to, FAR_NEAR)
        for o in (NEAR, SM, SP):
            send_table(rnd, peer[o], back[o])

    def compose(x):
        lane = x & (LANES - 1)
        row = x >> 7
        y = x
        for o in (FAR, NEAR, SM, SP):
            block = {FAR: far_block, NEAR: near_block, SM: 5, SP: 7}[o]
            for h in range(2):
                a, b = {FAR: (even, h), NEAR: (odd, h), SM: (h, 1), SP: (h, 0)}[o]
                for r in range(nrow):
                    line = got_send[o - 1, a, b : b + 1, cols_of(r)]
                    line = jnp.broadcast_to(line + o * nrow * LANES, x.shape)
                    y = jnp.where(row == (block + h) * nrow + r, lane_gather(line, lane), y)
        return y

    def compose_all():
        for o in (SP, SM, NEAR, FAR):
            landed(got_send.at[o - 1], recv_sem.at[1, o - 1])
        for i in range(srows):
            for r in range(nrow):
                sq[i * 8 : i * 8 + 8, cols_of(r)] = compose(sq[i * 8 : i * 8 + 8, cols_of(r)])
        remote(sq, gq, ghost_send.at[1], ghost_recv.at[1], peer[FAR])

    def compose_heads():
        for i in range(erow // 8):
            y = compose(head[i * 8 : i * 8 + 8, :])
            hq[i * 8 : i * 8 + 8, :] = y >> 7
            hl[i * 8 : i * 8 + 8, :] = y & (LANES - 1)

    def add_rows(rnd, slot, part, rows, lanes, accs):
        for i in range(len(rows)):
            for r in range(nrow):
                hit = rows[i] == part * nrow + r
                for k in range(4):
                    at = slot * vrow + k * nrow + r
                    line = jnp.broadcast_to(tab[rnd, at : at + 1, :], rows[i].shape)
                    v = lane_gather(line, lanes[i])
                    accs[i][k] = v if accs[i][k] is None else jnp.where(hit, v, accs[i][k])

    sub8 = lax.broadcasted_iota(I32, (8, LANES), 0)

    def fold(vecs):
        step = len(vecs) // 2
        while step:
            keep = (sub8 & step) == 0
            vecs = [
                jnp.where(keep, x, y) + pltpu.roll(jnp.where(keep, y, x), step, axis=0)
                if step == 4 else
                jnp.where(keep, x + pltpu.roll(x, 8 - step, axis=0), y + pltpu.roll(y, step, axis=0))
                for x, y in zip(vecs[:step], vecs[step:])
            ]
            step //= 2
        return vecs[0]

    tiles = [(slice(i * 8, i * 8 + 8), cols_of(r)) for i in range(srows) for r in range(nrow)]

    def sweep(rnd, index, factor, slots, start, out_slot, order, wait):
        where = [index[w] for w in tiles]
        rows = [y >> 7 for y in where]
        lanes = [y & (LANES - 1) for y in where]
        accs = [[None] * 4 for _ in tiles]
        for part in order:
            if part in wait:
                table_here(rnd, slots[part])
            add_rows(rnd, slots[part], part, rows, lanes, accs)
        totals = []
        for k in range(4):
            for r in range(nrow):
                total = None
                for i in range(srows):
                    n = i * nrow + r
                    v = accs[n][k] * factor[(k,) + tiles[n]]
                    total = v if total is None else total + v
                totals.append(total)
        for at in range(0, vrow, 8):
            to = out_slot * vrow + at
            tab[rnd + 1, to : to + 8, :] = start(at) - fold(totals[at : at + 8])

    def own_start(at):
        return bsc[at : at + 8, :]

    def ghost_start(at):
        return tab[0, FAR * vrow + at : FAR * vrow + at + 8, :]

    own_slots = (OWN, FAR, NEAR, SM, SP)
    for rnd in range(SWEEPS):
        deep = rnd % 2 == 0
        send_round(rnd, deep)
        if rnd == 0:
            compose_all()
        elif rnd == 1:
            compose_heads()
        if deep:
            sweep(rnd, sq, cf, own_slots, own_start, OWN, (OWN, SP, SM, NEAR, FAR), (SP, SM, NEAR, FAR))
        else:
            for slot in (FAR_NEAR, FAR_SM, FAR_SP):
                table_here(rnd - 1, slot)
            if rnd == 1:
                landed(gcf, ghost_recv.at[0])
                landed(gq, ghost_recv.at[1])
            sweep(rnd - 1, gq, gcf, GHOST_SLOT, ghost_start, FAR, (FAR, OWN, NEAR, SM, SP), ())
            if rnd < SWEEPS - 1:
                sweep(rnd, sq, cf, own_slots, own_start, OWN, (OWN, FAR, SP, SM, NEAR), (SP, SM, NEAR))

    last = SWEEPS - 1
    where = [slice(i * 8, i * 8 + 8) for i in range(erow // 8)]
    tails = [tail[w, :] for w in where]
    tacc = [[None] * 4 for _ in where]
    add_rows(last, OWN, OWN, [t >> 7 for t in tails], [t & (LANES - 1) for t in tails], tacc)
    rows = [hq[w, :] for w in where]
    lanes = [hl[w, :] for w in where]
    hacc = [[None] * 4 for _ in where]
    for part in (OWN, FAR, SP, SM, NEAR):
        if part in (SP, SM, NEAR):
            table_here(last, part)
        add_rows(last, part, part, rows, lanes, hacc)
    for i, w in enumerate(where):
        mixed = None
        for c in range(3):
            v = tan2[c * erow + i * 8 : c * erow + i * 8 + 8, :] * (tacc[i][c + 1] + hacc[i][c + 1])
            mixed = v if mixed is None else mixed + v
        out_ref[w, :] = scale[w, :] * res[w, :] + ((hacc[i][0] - tacc[i][0]) + 0.5 * mixed)

    for copy in started:
        copy.wait_send()


def body(
    residual, edge_scale, tangent, edge_tail, edge_head,
    stencil_index, stencil_coef, diag_margin, send_index,
):
    edges = residual.shape[0]
    erow = edges // LANES
    nodes = diag_margin.shape[1]
    nrow = nodes // LANES
    vrow = 4 * nrow
    stencil = stencil_index.shape[0]
    spad = -(-stencil // 8) * 8
    assert send_index.shape == (2, 2, nodes) and lax.axis_size("grp") % 2 == 0
    coef = jnp.transpose(stencil_coef, (1, 0, 2))
    square = lambda x: x.reshape(erow, LANES)
    anyspace = pl.BlockSpec(memory_space=pl.ANY)
    vm = pltpu.VMEM
    dma = pltpu.SemaphoreType.DMA
    out = pl.pallas_call(
        kernel,
        out_shape=vm((erow, LANES), F32),
        in_specs=[anyspace] * 9,
        out_specs=pl.BlockSpec(memory_space=vm),
        scratch_shapes=[
            vm((erow, LANES), F32),
            vm(tangent.shape, F32),
            vm((erow, LANES), I32),
            vm((erow, LANES), I32),
            vm(stencil_index.shape, I32),
            vm(coef.shape, BF16),
            vm(diag_margin.shape, F32),
            vm(send_index.shape, I32),
            vm((erow, LANES), F32),
            vm((4,) + send_index.shape, I32),
            vm((8 * vrow, LANES), F32),
            vm((8 * vrow, LANES), F32),
            vm((SWEEPS, SLOTS * vrow, LANES), F32),
            vm((LANES, edges), BF16),
            vm((2 * vrow, edges), BF16),
            vm((4 * vrow, edges), BF16),
            vm((14 * vrow, edges), BF16),
            vm((LANES, 4 * nodes), BF16),
            vm((2 * vrow, 4 * nodes), BF16),
            vm((4 * vrow, LANES), F32),
            vm((4, spad, nodes), F32),
            vm((4, spad, nodes), F32),
            vm((vrow, LANES), F32),
            vm((vrow, LANES), F32),
            vm((erow, LANES), I32),
            vm((erow, LANES), I32),
            vm((spad, nodes), I32),
            vm((spad, nodes), I32),
            vm((3 * erow, LANES), F32),
            dma((9,)),
            dma((2, 4)),
            dma((2, 4)),
            dma((SWEEPS, SLOTS - 1)),
            dma((SWEEPS, SLOTS - 1)),
            dma((2,)),
            dma((2,)),
        ],
        compiler_params=pltpu.CompilerParams(collective_id=0, has_side_effects=True),
    )(
        square(residual), tangent, square(edge_tail), square(edge_head),
        stencil_index, coef, diag_margin, send_index, square(edge_scale),
    )
    return out.reshape(edges)


def solution(mesh):
    return jax.shard_map(
        body,
        mesh=mesh,
        in_specs=(
            P(("grp", "sub")),
            P(("grp", "sub")),
            P(None, ("grp", "sub")),
            P(("grp", "sub")),
            P(("grp", "sub")),
            P(None, ("grp", "sub")),
            P(None, None, ("grp", "sub")),
            P(None, ("grp", "sub")),
            P("grp", "sub", None),
        ),
        out_specs=P(("grp", "sub")),
        check_vma=False,
    )
```

time: 30.9 us -> 28 us (0.906)
  the two profiles are of different devices: /device:TPU:0 before, /device:TPU:1 now
where the time goes in v1:
time: 28 us; the launch traced here: 27.8 us
  Pallas kernels  27.2 us (97%)
  local copies, waits for them, and re-layouts  0.6 us (2%)
    pallas_call x1, Pallas kernels, body(): pl.pallas_call(kernel, out_shape=vm((erow, LANES), F32), in_specs=[anyspa...  27.2 us
    unnamed x1, local copies, waits for them, and re-layouts  0.6 us

profile of v1, /device:TPU:1, one launch (start us, length us, event | category | flops | bytes accessed | tf_op | source)
XLA Modules:
  0.0 27.8 jit_solution(3200795805492153855)
XLA Ops:
  0.0 27.2 %shard_map.91 = f32[24,128]{1,0:T(8,128)S(1)} custom-call(f32[24,128]{1,0:T(8,128)} %bitcast.8, f32[3,3072]{1,0:T(4,128)} %tan_h.1, s32[24,128]{1,0:T(8,128)} %bitcast.9, s32[24,128]{1,0:T(8,128)} %bitcast.10, s32[14,512]{1,0:T(8,128)} %sidx_h.1, bf16[14,4,512]{2,1,0:T(4,128)(2,1)} %bitcast.7, f32[4,512]{1,0:T(4,128)} %marg_h.1, s32[2,2,512]{2,1,0:T(2,128)} %send_h.1, ...), custom_call_target="tpu_custom_call" | custom-call | tf_op jit(solution)/shard_map/pallas_call | solution.py:399
  27.2 0.6 %copy.11 = f32[3072]{0:T(1024)} copy(f32[3072]{0:T(1024)S(1)} %bitcast.6) | data formatting | bytes 24576

commit v2 on v1

--- a/solution.py
+++ b/solution.py
@@ -45,7 +45,7 @@
     res, tan, tail, head, sidx, coef, marg, own_send, scale,
     got_send, psend, got_p, tab, onehot, spread_o, spread_f, spread_r, onehot3, spread3, tsum,
     cf, gcf, bsc, diag, hq, hl, sq, gq, tan2,
-    local_sem, send_sem, recv_sem, tab_send, tab_recv, ghost_send, ghost_recv,
+    send_sem, recv_sem,
 ):
     G, S = lax.axis_size("grp"), lax.axis_size("sub")
     g, s = lax.axis_index("grp"), lax.axis_index("sub")
@@ -55,60 +55,64 @@
     sm, sp = lax.rem(s + S - 1, S), lax.rem(s + 1, S)
     peer = {FAR: (gf, s), NEAR: (gn, s), SM: (g, sm), SP: (g, sp)}
     nn_to = (lax.rem(g + 2 + (G - 4) * odd, G), s)
-    nn_from = (lax.rem(g + G - 2 + 4 * odd, G), s)
-    greeted = [peer[FAR], peer[NEAR], peer[SM], peer[SP], nn_to, nn_from, (gf, sm), (gf, sp)]
     back = {FAR: FAR, NEAR: NEAR, SM: SP, SP: SM}
     nrow = marg.shape[1] // LANES
     erow = res.shape[0]
     stencil = sidx.shape[0]
     vrow = 4 * nrow
     sent = 2 * vrow
-    srows = sq.shape[0] // 8
+    tiles = [slice(i * 8, i * 8 + 8) for i in range(sq.shape[0] // 8)]
 
     barrier = pltpu.get_barrier_semaphore()
-    for who in greeted:
-        pl.semaphore_signal(barrier, inc=1, device_id=who, device_id_type=MESH)
+    for o in (FAR, NEAR, SM, SP):
+        pl.semaphore_signal(barrier, inc=1, device_id=peer[o], device_id_type=MESH)
     pairs = (
-        (head_h, head), (res_h, res), (tan_h, tan), (send_h, own_send), (tail_h, tail),
-        (coef_h, coef), (marg_h, marg), (sidx_h, sidx), (scale_h, scale),
+        (head_h, head, 0), (res_h, res, 4), (tan_h, tan, 5), (send_h, own_send, 1), (tail_h, tail, 2),
+        (coef_h, coef, 3), (marg_h, marg, 6), (sidx_h, sidx, 7), (scale_h, scale, 8),
     )
-    local = [
-        pltpu.make_async_copy(src, dst, local_sem.at[i]) for i, (src, dst) in enumerate(pairs)
-    ]
+    local = [pltpu.make_async_copy(src, dst, send_sem.at[i]) for src, dst, i in pairs]
     for c in local:
         c.start()
 
-    started = []
-
-    def remote(src, dst, ssem, rsem, who):
-        copy = pltpu.make_async_remote_copy(
-            src_ref=src, dst_ref=dst, send_sem=ssem, recv_sem=rsem, device_id=who, device_id_type=MESH,
+    def copy_to(src, dst, ssem, rsem, who):
+        return pltpu.make_async_remote_copy(
+            src_ref=src, dst_ref=dst, send_sem=send_sem.at[ssem], recv_sem=recv_sem.at[rsem],
+            device_id=who, device_id_type=MESH,
         )
-        copy.start()
-        started.append(copy)
 
     def landed(dst, rsem):
-        pltpu.make_async_remote_copy(
-            src_ref=dst, dst_ref=dst, send_sem=rsem, recv_sem=rsem, device_id=peer[SP], device_id_type=MESH,
-        ).wait_recv()
+        copy_to(dst, dst, 0, rsem, peer[SP]).wait_recv()
+
+    def left(src, ssem):
+        copy_to(src, src, ssem, 0, peer[SP]).wait_send()
 
     def part_rows(ref, o):
         return ref.at[pl.ds((o - 1) * sent, sent)]
 
     def send_part(o):
-        remote(part_rows(psend, o), part_rows(got_p, back[o]), send_sem.at[0, o - 1], recv_sem.at[0, back[o] - 1], peer[o])
+        copy_to(part_rows(psend, o), part_rows(got_p, back[o]), 0, 0 if o == FAR else 1, peer[o]).start()
 
     def send_list(o):
-        remote(own_send, got_send.at[back[o] - 1], send_sem.at[1, o - 1], recv_sem.at[1, back[o] - 1], peer[o])
+        copy_to(own_send, got_send.at[back[o] - 1], 1, 2, peer[o]).start()
 
     def slot_rows(rnd, slot):
         return tab.at[rnd, pl.ds(slot * vrow, vrow)]
 
+    def group(rnd, slot):
+        if slot == FAR:
+            return 0
+        if slot > SP:
+            return 1
+        return 2 if rnd % 2 == 0 or slot > NEAR else 1
+
+    def table_sem(rnd, slot):
+        return 5 + (0, 3, 5, 8)[rnd] + group(rnd, slot) - rnd % 2
+
     def send_table(rnd, who, slot):
-        remote(slot_rows(rnd, OWN), slot_rows(rnd, slot), tab_send.at[rnd, slot - 1], tab_recv.at[rnd, slot - 1], who)
-
-    def table_here(rnd, slot):
-        landed(slot_rows(rnd, slot), tab_recv.at[rnd, slot - 1])
+        copy_to(slot_rows(rnd, OWN), slot_rows(rnd, slot), 4 + rnd, table_sem(rnd, slot), who).start()
+
+    def table_here(rnd, first, count=1):
+        landed(tab.at[rnd, pl.ds(first * vrow, count * vrow)], table_sem(rnd, first))
 
     riota = lax.broadcasted_iota(I32, (vrow, LANES), 0)
     kind = riota // nrow
@@ -162,26 +166,32 @@
 
     far_block, near_block = 1 + 2 * odd, 3 - 2 * odd
 
-    for c in local[:3]:
+    for c in local[:4]:
         c.wait()
     psend[0:sent] = scatter(spread_f, head, [base_of(far_block), base_of(far_block + 1)], 1, make=True)
-    pl.semaphore_wait(barrier, len(greeted))
-    send_part(FAR)
+
+    def first_sends():
+        pl.semaphore_wait(barrier, 4)
+        send_part(FAR)
+        for o in (FAR, NEAR, SM, SP):
+            send_list(o)
+
+    pl.when(g != 0)(first_sends)
     rest = scatter(
         spread_r, head,
         [base_of(b) for b in (near_block, near_block + 1, 5, 6, 7, 8, 0)], 1,
     )
     psend[sent:] = rest[: 3 * sent]
     own_sum = rest[3 * sent :]
+    pl.when(g == 0)(first_sends)
     for o in (NEAR, SM, SP):
         send_part(o)
-    local[3].wait()
-    for o in (FAR, NEAR, SM, SP):
-        send_list(o)
     for c in local[4:]:
         c.wait()
 
-    cf[...] = jnp.zeros_like(cf)
+    if cf.shape[1] > stencil * nrow:
+        cf[...] = jnp.zeros_like(cf)
+        sq[...] = jnp.zeros_like(sq)
     for k in range(4):
         for r in range(nrow):
             cols = cols_of(r)
@@ -189,8 +199,8 @@
             d = (1.0 + marg[k : k + 1, cols]) * jnp.sum(jnp.abs(c), axis=0, keepdims=True)
             inv = 1.0 / d
             diag[k * nrow + r : k * nrow + r + 1, :] = inv
-            cf[k, :stencil, cols] = c * inv
-    remote(cf, gcf, ghost_send.at[0], ghost_recv.at[0], peer[FAR])
+            cf[k, pl.ds(r, stencil, stride=nrow), :] = c * inv
+    copy_to(cf, gcf, 2, 3, peer[FAR]).start()
 
     for t in range(erow):
         lanes_onehot(onehot, cols_of(t), tail[t : t + 1, :])
@@ -207,8 +217,8 @@
     for c in range(3):
         for t in range(erow):
             tan2[c * erow + t : c * erow + t + 1, :] = tan[c : c + 1, cols_of(t)]
-    sq[...] = jnp.zeros_like(sq)
-    sq[:stencil, :] = sidx[...]
+    for r in range(nrow):
+        sq[pl.ds(r, stencil, stride=nrow), :] = sidx[:, cols_of(r)]
 
     def place(ref, at, f, b, r):
         hit = wide(own_list(f, b, r) >> 7, vrow) == rpart
@@ -219,8 +229,7 @@
             val = jnp.where(kind == k, ref[row : row + 1, :], val)
         return [jnp.where(hit, v, zero) for v in split(val)]
 
-    for o in (SP, SM, NEAR):
-        landed(part_rows(got_p, o), recv_sem.at[0, o - 1])
+    landed(got_p.at[pl.ds(sent, 3 * sent)], 1)
     for f in range(2):
         for b in range(2):
             first = pl.multiple_of((2 + b) * sent + a_of[f] * vrow, vrow)
@@ -235,7 +244,7 @@
     got = nt_dot(spread3[...], onehot3[...])
     own_sum = own_sum + (got[:vrow] + got[vrow:])
 
-    landed(part_rows(got_p, FAR), recv_sem.at[0, FAR - 1])
+    landed(part_rows(got_p, FAR), 0)
     half = len(lists) // 2
     for n, (f, b, r) in enumerate(lists[:half]):
         for p, v in enumerate(place(got_p, 0, f, b, r)):
@@ -268,12 +277,10 @@
         return y
 
     def compose_all():
-        for o in (SP, SM, NEAR, FAR):
-            landed(got_send.at[o - 1], recv_sem.at[1, o - 1])
-        for i in range(srows):
-            for r in range(nrow):
-                sq[i * 8 : i * 8 + 8, cols_of(r)] = compose(sq[i * 8 : i * 8 + 8, cols_of(r)])
-        remote(sq, gq, ghost_send.at[1], ghost_recv.at[1], peer[FAR])
+        landed(got_send, 2)
+        for w in tiles:
+            sq[w, :] = compose(sq[w, :])
+        copy_to(sq, gq, 3, 4, peer[FAR]).start()
 
     def compose_heads():
         for i in range(erow // 8):
@@ -293,42 +300,32 @@
 
     sub8 = lax.broadcasted_iota(I32, (8, LANES), 0)
 
-    def fold(vecs):
-        step = len(vecs) // 2
-        while step:
-            keep = (sub8 & step) == 0
-            vecs = [
-                jnp.where(keep, x, y) + pltpu.roll(jnp.where(keep, y, x), step, axis=0)
-                if step == 4 else
-                jnp.where(keep, x + pltpu.roll(x, 8 - step, axis=0), y + pltpu.roll(y, step, axis=0))
-                for x, y in zip(vecs[:step], vecs[step:])
-            ]
-            step //= 2
-        return vecs[0]
-
-    tiles = [(slice(i * 8, i * 8 + 8), cols_of(r)) for i in range(srows) for r in range(nrow)]
-
     def sweep(rnd, index, factor, slots, start, out_slot, order, wait):
-        where = [index[w] for w in tiles]
+        where = [index[w, :] for w in tiles]
         rows = [y >> 7 for y in where]
         lanes = [y & (LANES - 1) for y in where]
         accs = [[None] * 4 for _ in tiles]
         for part in order:
             if part in wait:
-                table_here(rnd, slots[part])
+                table_here(rnd, *wait[part])
             add_rows(rnd, slots[part], part, rows, lanes, accs)
         totals = []
         for k in range(4):
-            for r in range(nrow):
-                total = None
-                for i in range(srows):
-                    n = i * nrow + r
-                    v = accs[n][k] * factor[(k,) + tiles[n]]
-                    total = v if total is None else total + v
-                totals.append(total)
+            total = None
+            for w, acc in zip(tiles, accs):
+                v = acc[k] * factor[k, w, :]
+                total = v if total is None else total + v
+            step = nrow
+            while step < 8:
+                total = total + pltpu.roll(total, step, axis=0)
+                step *= 2
+            totals.append(total)
         for at in range(0, vrow, 8):
+            total = totals[at // nrow]
+            for m in range(1, 8 // nrow):
+                total = jnp.where(sub8 >= m * nrow, totals[at // nrow + m], total)
             to = out_slot * vrow + at
-            tab[rnd + 1, to : to + 8, :] = start(at) - fold(totals[at : at + 8])
+            tab[rnd + 1, to : to + 8, :] = start(at) - total
 
     def own_start(at):
         return bsc[at : at + 8, :]
@@ -345,16 +342,21 @@
         elif rnd == 1:
             compose_heads()
         if deep:
-            sweep(rnd, sq, cf, own_slots, own_start, OWN, (OWN, SP, SM, NEAR, FAR), (SP, SM, NEAR, FAR))
+            sweep(
+                rnd, sq, cf, own_slots, own_start, OWN,
+                (OWN, SP, SM, NEAR, FAR), {SP: (NEAR, 3), FAR: (FAR, 1)},
+            )
         else:
-            for slot in (FAR_NEAR, FAR_SM, FAR_SP):
-                table_here(rnd - 1, slot)
+            table_here(rnd - 1, FAR_NEAR, 3)
             if rnd == 1:
-                landed(gcf, ghost_recv.at[0])
-                landed(gq, ghost_recv.at[1])
-            sweep(rnd - 1, gq, gcf, GHOST_SLOT, ghost_start, FAR, (FAR, OWN, NEAR, SM, SP), ())
+                landed(gcf, 3)
+                landed(gq, 4)
+            sweep(rnd - 1, gq, gcf, GHOST_SLOT, ghost_start, FAR, (FAR, OWN, NEAR, SM, SP), {})
             if rnd < SWEEPS - 1:
-                sweep(rnd, sq, cf, own_slots, own_start, OWN, (OWN, FAR, SP, SM, NEAR), (SP, SM, NEAR))
+                sweep(
+                    rnd, sq, cf, own_slots, own_start, OWN,
+                    (OWN, FAR, SP, SM, NEAR), {SP: (SM, 2), NEAR: (NEAR, 1)},
+                )
 
     last = SWEEPS - 1
     where = [slice(i * 8, i * 8 + 8) for i in range(erow // 8)]
@@ -365,8 +367,10 @@
     lanes = [hl[w, :] for w in where]
     hacc = [[None] * 4 for _ in where]
     for part in (OWN, FAR, SP, SM, NEAR):
-        if part in (SP, SM, NEAR):
-            table_here(last, part)
+        if part == SP:
+            table_here(last, SM, 2)
+        elif part == NEAR:
+            table_here(last, NEAR)
         add_rows(last, part, part, rows, lanes, hacc)
     for i, w in enumerate(where):
         mixed = None
@@ -375,8 +379,12 @@
             mixed = v if mixed is None else mixed + v
         out_ref[w, :] = scale[w, :] * res[w, :] + ((hacc[i][0] - tacc[i][0]) + 0.5 * mixed)
 
-    for copy in started:
-        copy.wait_send()
+    left(psend, 0)
+    left(got_send, 1)
+    left(cf, 2)
+    left(sq, 3)
+    for rnd in range(SWEEPS):
+        left(tab.at[rnd, pl.ds(0, (7 if rnd % 2 == 0 else 3) * vrow)], 4 + rnd)
 
 
 def body(
@@ -389,7 +397,7 @@
     nrow = nodes // LANES
     vrow = 4 * nrow
     stencil = stencil_index.shape[0]
-    spad = -(-stencil // 8) * 8
+    qrow = -(-stencil * nrow // 8) * 8
     assert send_index.shape == (2, 2, nodes) and lax.axis_size("grp") % 2 == 0
     coef = jnp.transpose(stencil_coef, (1, 0, 2))
     square = lambda x: x.reshape(erow, LANES)
@@ -422,22 +430,17 @@
             vm((LANES, 4 * nodes), BF16),
             vm((2 * vrow, 4 * nodes), BF16),
             vm((4 * vrow, LANES), F32),
-            vm((4, spad, nodes), F32),
-            vm((4, spad, nodes), F32),
+            vm((4, qrow, LANES), F32),
+            vm((4, qrow, LANES), F32),
             vm((vrow, LANES), F32),
             vm((vrow, LANES), F32),
             vm((erow, LANES), I32),
             vm((erow, LANES), I32),
-            vm((spad, nodes), I32),
-            vm((spad, nodes), I32),
+            vm((qrow, LANES), I32),
+            vm((qrow, LANES), I32),
             vm((3 * erow, LANES), F32),
             dma((9,)),
-            dma((2, 4)),
-            dma((2, 4)),
-            dma((SWEEPS, SLOTS - 1)),
-            dma((SWEEPS, SLOTS - 1)),
-            dma((2,)),
-            dma((2,)),
+            dma((15,)),
         ],
         compiler_params=pltpu.CompilerParams(collective_id=0, has_side_effects=True),
     )(

time: 28 us -> 25.4 us (0.907)
  Pallas kernels: 27.2 us -> 24.5 us
    pallas_call x1, Pallas kernels: 27.2 us -> 24.5 us  [body(): pl.pallas_call(kernel, out_shape=vm((erow, LANES), F32), in_specs=[anyspa...]
where the time goes in v2:
time: 25.4 us; the launch traced here: 25.1 us
  Pallas kernels  24.5 us (96%)
  local copies, waits for them, and re-layouts  0.6 us (2%)
    pallas_call x1, Pallas kernels, body(): pl.pallas_call(kernel, out_shape=vm((erow, LANES), F32), in_specs=[anyspa...  24.5 us
    unnamed x1, local copies, waits for them, and re-layouts  0.6 us

profile of v2, /device:TPU:1, one launch (start us, length us, event | category | flops | bytes accessed | tf_op | source)
XLA Modules:
  0.0 25.1 jit_solution(13804006760523598370)
XLA Ops:
  0.0 24.5 %shard_map.91 = f32[24,128]{1,0:T(8,128)S(1)} custom-call(f32[24,128]{1,0:T(8,128)} %bitcast.8, f32[3,3072]{1,0:T(4,128)} %tan_h.1, s32[24,128]{1,0:T(8,128)} %bitcast.9, s32[24,128]{1,0:T(8,128)} %bitcast.10, s32[14,512]{1,0:T(8,128)} %sidx_h.1, bf16[14,4,512]{2,1,0:T(4,128)(2,1)} %bitcast.7, f32[4,512]{1,0:T(4,128)} %marg_h.1, s32[2,2,512]{2,1,0:T(2,128)} %send_h.1, ...), custom_call_target="tpu_custom_call" | custom-call | tf_op jit(solution)/shard_map/pallas_call | solution.py:407
  24.5 0.6 %copy.11 = f32[3072]{0:T(1024)} copy(f32[3072]{0:T(1024)S(1)} %bitcast.6) | data formatting | bytes 24576

commit v3 on v2

--- a/solution.py
+++ b/solution.py
@@ -90,7 +90,8 @@
         return ref.at[pl.ds((o - 1) * sent, sent)]
 
     def send_part(o):
-        copy_to(part_rows(psend, o), part_rows(got_p, back[o]), 0, 0 if o == FAR else 1, peer[o]).start()
+        far = o == FAR
+        copy_to(part_rows(psend, o), part_rows(got_p, back[o]), 9 if far else 0, 0 if far else 1, peer[o]).start()
 
     def send_list(o):
         copy_to(own_send, got_send.at[back[o] - 1], 1, 2, peer[o]).start()
@@ -98,15 +99,9 @@
     def slot_rows(rnd, slot):
         return tab.at[rnd, pl.ds(slot * vrow, vrow)]
 
-    def group(rnd, slot):
-        if slot == FAR:
-            return 0
-        if slot > SP:
-            return 1
-        return 2 if rnd % 2 == 0 or slot > NEAR else 1
-
     def table_sem(rnd, slot):
-        return 5 + (0, 3, 5, 8)[rnd] + group(rnd, slot) - rnd % 2
+        own = slot + 3 if rnd % 2 else min(slot, FAR_NEAR) - 1 if isinstance(slot, int) else slot - 1
+        return 5 + SLOTS * (rnd // 2) + own
 
     def send_table(rnd, who, slot):
         copy_to(slot_rows(rnd, OWN), slot_rows(rnd, slot), 4 + rnd, table_sem(rnd, slot), who).start()
@@ -200,7 +195,6 @@
             inv = 1.0 / d
             diag[k * nrow + r : k * nrow + r + 1, :] = inv
             cf[k, pl.ds(r, stencil, stride=nrow), :] = c * inv
-    copy_to(cf, gcf, 2, 3, peer[FAR]).start()
 
     for t in range(erow):
         lanes_onehot(onehot, cols_of(t), tail[t : t + 1, :])
@@ -229,6 +223,9 @@
             val = jnp.where(kind == k, ref[row : row + 1, :], val)
         return [jnp.where(hit, v, zero) for v in split(val)]
 
+    parts_left = lambda: left(psend.at[pl.ds(sent, 3 * sent)], 0)
+    pl.when(g != 0)(parts_left)
+    copy_to(cf, gcf, 2, 3, peer[FAR]).start()
     landed(got_p.at[pl.ds(sent, 3 * sent)], 1)
     for f in range(2):
         for b in range(2):
@@ -256,11 +253,12 @@
     def send_round(rnd, deep):
         if deep:
             send_table(rnd, peer[FAR], FAR)
+        for o in (NEAR, SM, SP):
+            send_table(rnd, peer[o], back[o])
+        if deep:
             send_table(rnd, (gf, sp), FAR_SM)
             send_table(rnd, (gf, sm), FAR_SP)
             send_table(rnd, nn_to, FAR_NEAR)
-        for o in (NEAR, SM, SP):
-            send_table(rnd, peer[o], back[o])
 
     def compose(x):
         lane = x & (LANES - 1)
@@ -294,21 +292,24 @@
                 hit = rows[i] == part * nrow + r
                 for k in range(4):
                     at = slot * vrow + k * nrow + r
-                    line = jnp.broadcast_to(tab[rnd, at : at + 1, :], rows[i].shape)
+                    line = jnp.broadcast_to(tab[rnd, pl.ds(at, 1), :], rows[i].shape)
                     v = lane_gather(line, lanes[i])
                     accs[i][k] = v if accs[i][k] is None else jnp.where(hit, v, accs[i][k])
 
     sub8 = lax.broadcasted_iota(I32, (8, LANES), 0)
 
-    def sweep(rnd, index, factor, slots, start, out_slot, order, wait):
+    def open_sweep(rnd, index):
         where = [index[w, :] for w in tiles]
         rows = [y >> 7 for y in where]
         lanes = [y & (LANES - 1) for y in where]
         accs = [[None] * 4 for _ in tiles]
-        for part in order:
-            if part in wait:
-                table_here(rnd, *wait[part])
-            add_rows(rnd, slots[part], part, rows, lanes, accs)
+
+        def add(part, slot=None):
+            add_rows(rnd, part if slot is None else slot, part, rows, lanes, accs)
+
+        return add, accs
+
+    def close_sweep(rnd, accs, factor, start, out_slot):
         totals = []
         for k in range(4):
             total = None
@@ -333,45 +334,55 @@
     def ghost_start(at):
         return tab[0, FAR * vrow + at : FAR * vrow + at + 8, :]
 
-    own_slots = (OWN, FAR, NEAR, SM, SP)
-    for rnd in range(SWEEPS):
-        deep = rnd % 2 == 0
-        send_round(rnd, deep)
+    s_odd = lax.rem(s, 2)
+    arrivals = (SP - s_odd, SM - s_odd, NEAR + 2 * s_odd)
+
+    for rnd in range(0, SWEEPS, 2):
+        send_round(rnd, True)
         if rnd == 0:
             compose_all()
-        elif rnd == 1:
             compose_heads()
-        if deep:
-            sweep(
-                rnd, sq, cf, own_slots, own_start, OWN,
-                (OWN, SP, SM, NEAR, FAR), {SP: (NEAR, 3), FAR: (FAR, 1)},
-            )
+        add, accs = open_sweep(rnd, sq)
+        add(OWN)
+        for part in arrivals + (FAR,):
+            table_here(rnd, part)
+            add(part)
+        close_sweep(rnd, accs, cf, own_start, OWN)
+        send_round(rnd + 1, False)
+
+        final = rnd + 2 == SWEEPS
+        if final:
+            where = [slice(i * 8, i * 8 + 8) for i in range(erow // 8)]
+            tails = [tail[w, :] for w in where]
+            tacc = [[None] * 4 for _ in where]
+            add_rows(rnd + 1, OWN, OWN, [t >> 7 for t in tails], [t & (LANES - 1) for t in tails], tacc)
+            rows = [hq[w, :] for w in where]
+            lanes = [hl[w, :] for w in where]
+            hacc = [[None] * 4 for _ in where]
+
+            def add(part):
+                add_rows(rnd + 1, part, part, rows, lanes, hacc)
         else:
-            table_here(rnd - 1, FAR_NEAR, 3)
-            if rnd == 1:
-                landed(gcf, 3)
-                landed(gq, 4)
-            sweep(rnd - 1, gq, gcf, GHOST_SLOT, ghost_start, FAR, (FAR, OWN, NEAR, SM, SP), {})
-            if rnd < SWEEPS - 1:
-                sweep(
-                    rnd, sq, cf, own_slots, own_start, OWN,
-                    (OWN, FAR, SP, SM, NEAR), {SP: (SM, 2), NEAR: (NEAR, 1)},
-                )
-
-    last = SWEEPS - 1
-    where = [slice(i * 8, i * 8 + 8) for i in range(erow // 8)]
-    tails = [tail[w, :] for w in where]
-    tacc = [[None] * 4 for _ in where]
-    add_rows(last, OWN, OWN, [t >> 7 for t in tails], [t & (LANES - 1) for t in tails], tacc)
-    rows = [hq[w, :] for w in where]
-    lanes = [hl[w, :] for w in where]
-    hacc = [[None] * 4 for _ in where]
-    for part in (OWN, FAR, SP, SM, NEAR):
-        if part == SP:
-            table_here(last, SM, 2)
-        elif part == NEAR:
-            table_here(last, NEAR)
-        add_rows(last, part, part, rows, lanes, hacc)
+            add, accs = open_sweep(rnd + 1, sq)
+        add(OWN)
+        if rnd == 0:
+            landed(gq, 4)
+        ghost_add, ghost_accs = open_sweep(rnd, gq)
+        ghost_add(OWN, FAR)
+        ghost_add(FAR, OWN)
+        table_here(rnd, FAR_NEAR, 3)
+        for part in (NEAR, SM, SP):
+            ghost_add(part, GHOST_SLOT[part])
+        if rnd == 0:
+            landed(gcf, 3)
+        close_sweep(rnd, ghost_accs, gcf, ghost_start, FAR)
+        add(FAR)
+        for part in arrivals:
+            table_here(rnd + 1, part)
+            add(part)
+        if not final:
+            close_sweep(rnd + 1, accs, cf, own_start, OWN)
+
     for i, w in enumerate(where):
         mixed = None
         for c in range(3):
@@ -379,7 +390,8 @@
             mixed = v if mixed is None else mixed + v
         out_ref[w, :] = scale[w, :] * res[w, :] + ((hacc[i][0] - tacc[i][0]) + 0.5 * mixed)
 
-    left(psend, 0)
+    pl.when(g == 0)(parts_left)
+    left(part_rows(psend, FAR), 9)
     left(got_send, 1)
     left(cf, 2)
     left(sq, 3)
@@ -439,8 +451,8 @@
             vm((qrow, LANES), I32),
             vm((qrow, LANES), I32),
             vm((3 * erow, LANES), F32),
-            dma((9,)),
-            dma((15,)),
+            dma((10,)),
+            dma((5 + SLOTS * (SWEEPS // 2),)),
         ],
         compiler_params=pltpu.CompilerParams(collective_id=0, has_side_effects=True),
     )(

time: 25.4 us -> 24.4 us (0.961)
  Pallas kernels: 24.5 us -> 23.6 us
    pallas_call x1, Pallas kernels: 24.5 us -> 23.6 us  [body(): pl.pallas_call(kernel, out_shape=vm((erow, LANES), F32), in_specs=[anyspa...]
where the time goes in v3:
time: 24.4 us; the launch traced here: 24.2 us
  Pallas kernels  23.6 us (97%)
  local copies, waits for them, and re-layouts  0.6 us (2%)
    pallas_call x1, Pallas kernels, body(): pl.pallas_call(kernel, out_shape=vm((erow, LANES), F32), in_specs=[anyspa...  23.6 us
    unnamed x1, local copies, waits for them, and re-layouts  0.6 us

profile of v3, /device:TPU:1, one launch (start us, length us, event | category | flops | bytes accessed | tf_op | source)
XLA Modules:
  0.0 24.2 jit_solution(17818718137835213516)
XLA Ops:
  0.0 23.6 %shard_map.91 = f32[24,128]{1,0:T(8,128)S(1)} custom-call(f32[24,128]{1,0:T(8,128)} %bitcast.8, f32[3,3072]{1,0:T(4,128)} %tan_h.1, s32[24,128]{1,0:T(8,128)} %bitcast.9, s32[24,128]{1,0:T(8,128)} %bitcast.10, s32[14,512]{1,0:T(8,128)} %sidx_h.1, bf16[14,4,512]{2,1,0:T(4,128)(2,1)} %bitcast.7, f32[4,512]{1,0:T(4,128)} %marg_h.1, s32[2,2,512]{2,1,0:T(2,128)} %send_h.1, ...), custom_call_target="tpu_custom_call" | custom-call | tf_op jit(solution)/shard_map/pallas_call | solution.py:419
  23.6 0.6 %copy.11 = f32[3072]{0:T(1024)} copy(f32[3072]{0:T(1024)S(1)} %bitcast.6) | data formatting | bytes 24576

commit v4 on v3

--- a/solution.py
+++ b/solution.py
@@ -55,6 +55,10 @@
     sm, sp = lax.rem(s + S - 1, S), lax.rem(s + 1, S)
     peer = {FAR: (gf, s), NEAR: (gn, s), SM: (g, sm), SP: (g, sp)}
     nn_to = (lax.rem(g + 2 + (G - 4) * odd, G), s)
+    seam = (g == 0) | (g == G - 1)
+    plain = (g != 0) & (g != G - 1)
+    feeds = (g == 1) | (g == G - 2)
+    inner = plain & (g != 1) & (g != G - 2)
     back = {FAR: FAR, NEAR: NEAR, SM: SP, SP: SM}
     nrow = marg.shape[1] // LANES
     erow = res.shape[0]
@@ -100,8 +104,8 @@
         return tab.at[rnd, pl.ds(slot * vrow, vrow)]
 
     def table_sem(rnd, slot):
-        own = slot + 3 if rnd % 2 else min(slot, FAR_NEAR) - 1 if isinstance(slot, int) else slot - 1
-        return 5 + SLOTS * (rnd // 2) + own
+        slot = min(slot, FAR_NEAR) if isinstance(slot, int) else slot
+        return 5 + 9 * (rnd // 2) + slot - 1 + FAR_NEAR * (rnd % 2)
 
     def send_table(rnd, who, slot):
         copy_to(slot_rows(rnd, OWN), slot_rows(rnd, slot), 4 + rnd, table_sem(rnd, slot), who).start()
@@ -224,8 +228,12 @@
         return [jnp.where(hit, v, zero) for v in split(val)]
 
     parts_left = lambda: left(psend.at[pl.ds(sent, 3 * sent)], 0)
-    pl.when(g != 0)(parts_left)
-    copy_to(cf, gcf, 2, 3, peer[FAR]).start()
+    pl.when(g == G - 1)(parts_left)
+
+    @pl.when(seam)
+    def _():
+        copy_to(cf, gcf, 2, 3, peer[FAR]).start()
+
     landed(got_p.at[pl.ds(sent, 3 * sent)], 1)
     for f in range(2):
         for b in range(2):
@@ -256,9 +264,18 @@
         for o in (NEAR, SM, SP):
             send_table(rnd, peer[o], back[o])
         if deep:
-            send_table(rnd, (gf, sp), FAR_SM)
-            send_table(rnd, (gf, sm), FAR_SP)
-            send_table(rnd, nn_to, FAR_NEAR)
+            @pl.when(seam)
+            def _():
+                send_table(rnd, (gf, sp), FAR_SM)
+                send_table(rnd, (gf, sm), FAR_SP)
+
+            @pl.when(feeds)
+            def _():
+                send_table(rnd, nn_to, FAR_NEAR)
+        else:
+            @pl.when(plain)
+            def _():
+                send_table(rnd, peer[FAR], FAR)
 
     def compose(x):
         lane = x & (LANES - 1)
@@ -278,7 +295,10 @@
         landed(got_send, 2)
         for w in tiles:
             sq[w, :] = compose(sq[w, :])
-        copy_to(sq, gq, 3, 4, peer[FAR]).start()
+
+        @pl.when(seam)
+        def _():
+            copy_to(sq, gq, 3, 4, peer[FAR]).start()
 
     def compose_heads():
         for i in range(erow // 8):
@@ -335,7 +355,17 @@
         return tab[0, FAR * vrow + at : FAR * vrow + at + 8, :]
 
     s_odd = lax.rem(s, 2)
-    arrivals = (SP - s_odd, SM - s_odd, NEAR + 2 * s_odd)
+    partner, across = SP - s_odd, SM + s_odd
+    second, third = SM - s_odd, NEAR + 2 * s_odd
+
+    def either(here, there):
+        return [jnp.where(seam, a, b) for a, b in zip(here, there)]
+
+    slow_order = (
+        either((partner, second, third, FAR), (partner, across, FAR, NEAR)),
+        either((partner, second, FAR, third), (partner, across, FAR, NEAR)),
+    )
+    fast_order = either((FAR, partner, second, third), (partner, across, FAR, NEAR))
 
     for rnd in range(0, SWEEPS, 2):
         send_round(rnd, True)
@@ -344,7 +374,7 @@
             compose_heads()
         add, accs = open_sweep(rnd, sq)
         add(OWN)
-        for part in arrivals + (FAR,):
+        for part in slow_order[rnd // 2]:
             table_here(rnd, part)
             add(part)
         close_sweep(rnd, accs, cf, own_start, OWN)
@@ -365,20 +395,28 @@
         else:
             add, accs = open_sweep(rnd + 1, sq)
         add(OWN)
-        if rnd == 0:
-            landed(gq, 4)
-        ghost_add, ghost_accs = open_sweep(rnd, gq)
-        ghost_add(OWN, FAR)
-        ghost_add(FAR, OWN)
-        table_here(rnd, FAR_NEAR, 3)
-        for part in (NEAR, SM, SP):
-            ghost_add(part, GHOST_SLOT[part])
-        if rnd == 0:
-            landed(gcf, 3)
-        close_sweep(rnd, ghost_accs, gcf, ghost_start, FAR)
-        add(FAR)
-        for part in arrivals:
-            table_here(rnd + 1, part)
+
+        @pl.when(seam)
+        def _():
+            if rnd == 0:
+                landed(gq, 4)
+            ghost_add, ghost_accs = open_sweep(rnd, gq)
+            ghost_add(OWN, FAR)
+            ghost_add(FAR, OWN)
+            table_here(rnd, FAR_NEAR, 3)
+            for part in (NEAR, SM, SP):
+                ghost_add(part, GHOST_SLOT[part])
+            if rnd == 0:
+                landed(gcf, 3)
+            close_sweep(rnd, ghost_accs, gcf, ghost_start, FAR)
+
+        @pl.when(plain)
+        def _():
+            table_here(rnd + 1, partner)
+
+        for n, part in enumerate(fast_order):
+            if n:
+                table_here(rnd + 1, part)
             add(part)
         if not final:
             close_sweep(rnd + 1, accs, cf, own_start, OWN)
@@ -390,13 +428,19 @@
             mixed = v if mixed is None else mixed + v
         out_ref[w, :] = scale[w, :] * res[w, :] + ((hacc[i][0] - tacc[i][0]) + 0.5 * mixed)
 
-    pl.when(g == 0)(parts_left)
+    pl.when(g != G - 1)(parts_left)
     left(part_rows(psend, FAR), 9)
     left(got_send, 1)
-    left(cf, 2)
-    left(sq, 3)
+
+    @pl.when(seam)
+    def _():
+        left(cf, 2)
+        left(sq, 3)
+
     for rnd in range(SWEEPS):
-        left(tab.at[rnd, pl.ds(0, (7 if rnd % 2 == 0 else 3) * vrow)], 4 + rnd)
+        counts = ((inner, 4), (feeds, 5), (seam, 6)) if rnd % 2 == 0 else ((plain, 4), (seam, 3))
+        for which, n in counts:
+            pl.when(which)(lambda n=n: left(tab.at[rnd, pl.ds(0, n * vrow)], 4 + rnd))
 
 
 def body(
@@ -410,7 +454,7 @@
     vrow = 4 * nrow
     stencil = stencil_index.shape[0]
     qrow = -(-stencil * nrow // 8) * 8
-    assert send_index.shape == (2, 2, nodes) and lax.axis_size("grp") % 2 == 0
+    assert send_index.shape == (2, 2, nodes) and lax.axis_size("grp") % 2 == 0 and lax.axis_size("grp") > 4
     coef = jnp.transpose(stencil_coef, (1, 0, 2))
     square = lambda x: x.reshape(erow, LANES)
     anyspace = pl.BlockSpec(memory_space=pl.ANY)
@@ -452,7 +496,7 @@
             vm((qrow, LANES), I32),
             vm((3 * erow, LANES), F32),
             dma((10,)),
-            dma((5 + SLOTS * (SWEEPS // 2),)),
+            dma((5 + 9 * (SWEEPS // 2),)),
         ],
         compiler_params=pltpu.CompilerParams(collective_id=0, has_side_effects=True),
     )(

time: 24.4 us -> 24.4 us (level)
  no operation moved by 1% of the time
where the time goes in v4:
time: 24.4 us; the launch traced here: 24.2 us
  Pallas kernels  23.6 us (97%)
  local copies, waits for them, and re-layouts  0.6 us (2%)
    pallas_call x1, Pallas kernels, body(): pl.pallas_call(kernel, out_shape=vm((erow, LANES), F32), in_specs=[anyspa...  23.6 us
    unnamed x1, local copies, waits for them, and re-layouts  0.6 us

profile of v4, /device:TPU:1, one launch (start us, length us, event | category | flops | bytes accessed | tf_op | source)
XLA Modules:
  0.0 24.2 jit_solution(6948658117750265199)
XLA Ops:
  0.0 23.6 %shard_map.91 = f32[24,128]{1,0:T(8,128)S(1)} custom-call(f32[24,128]{1,0:T(8,128)} %bitcast.8, f32[3,3072]{1,0:T(4,128)} %tan_h.1, s32[24,128]{1,0:T(8,128)} %bitcast.9, s32[24,128]{1,0:T(8,128)} %bitcast.10, s32[14,512]{1,0:T(8,128)} %sidx_h.1, bf16[14,4,512]{2,1,0:T(4,128)(2,1)} %bitcast.7, f32[4,512]{1,0:T(4,128)} %marg_h.1, s32[2,2,512]{2,1,0:T(2,128)} %send_h.1, ...), custom_call_target="tpu_custom_call" | custom-call | tf_op jit(solution)/shard_map/pallas_call | solution.py:463
  23.6 0.6 %copy.11 = f32[3072]{0:T(1024)} copy(f32[3072]{0:T(1024)S(1)} %bitcast.6) | data formatting | bytes 24576

commit v5 on v4

--- a/solution.py
+++ b/solution.py
@@ -44,7 +44,7 @@
     out_ref,
     res, tan, tail, head, sidx, coef, marg, own_send, scale,
     got_send, psend, got_p, tab, onehot, spread_o, spread_f, spread_r, onehot3, spread3, tsum,
-    cf, gcf, bsc, diag, hq, hl, sq, gq, tan2,
+    cf, gcf, bsc, diag, hq, hl, sq, gq, sidx2, gacc, tan2, relay_p, relay_l,
     send_sem, recv_sem,
 ):
     G, S = lax.axis_size("grp"), lax.axis_size("sub")
@@ -59,6 +59,13 @@
     plain = (g != 0) & (g != G - 1)
     feeds = (g == 1) | (g == G - 2)
     inner = plain & (g != 1) & (g != G - 2)
+    s_odd = lax.rem(s, 2)
+    paired = (g, s + 1 - 2 * s_odd)
+    lead = (g == 0) & (s_odd == 0)
+    led = (g != 0) | (s_odd != 0)
+    aide = (g == 0) & (s_odd == 1)
+    far_aide = (g == G - 1) & (s_odd == 1)
+    either_aide = seam & (s_odd == 1)
     back = {FAR: FAR, NEAR: NEAR, SM: SP, SP: SM}
     nrow = marg.shape[1] // LANES
     erow = res.shape[0]
@@ -68,8 +75,13 @@
     tiles = [slice(i * 8, i * 8 + 8) for i in range(sq.shape[0] // 8)]
 
     barrier = pltpu.get_barrier_semaphore()
-    for o in (FAR, NEAR, SM, SP):
+    for o in (NEAR, SM, SP):
         pl.semaphore_signal(barrier, inc=1, device_id=peer[o], device_id_type=MESH)
+
+    skip = (g == G - 1) & (s_odd == 0)
+    greeted = (jnp.where(skip, lax.rem(g + 2, G), gf), s)
+    pl.semaphore_signal(barrier, inc=1, device_id=greeted, device_id_type=MESH)
+
     pairs = (
         (head_h, head, 0), (res_h, res, 4), (tan_h, tan, 5), (send_h, own_send, 1), (tail_h, tail, 2),
         (coef_h, coef, 3), (marg_h, marg, 6), (sidx_h, sidx, 7), (scale_h, scale, 8),
@@ -98,7 +110,7 @@
         copy_to(part_rows(psend, o), part_rows(got_p, back[o]), 9 if far else 0, 0 if far else 1, peer[o]).start()
 
     def send_list(o):
-        copy_to(own_send, got_send.at[back[o] - 1], 1, 2, peer[o]).start()
+        copy_to(own_send, got_send.at[back[o] - 1], 1, 25 if o == FAR else 2, peer[o]).start()
 
     def slot_rows(rnd, slot):
         return tab.at[rnd, pl.ds(slot * vrow, vrow)]
@@ -170,9 +182,27 @@
     psend[0:sent] = scatter(spread_f, head, [base_of(far_block), base_of(far_block + 1)], 1, make=True)
 
     def first_sends():
-        pl.semaphore_wait(barrier, 4)
-        send_part(FAR)
-        for o in (FAR, NEAR, SM, SP):
+        extra = (g == 1) & (s_odd == 0)
+        pl.semaphore_wait(barrier, jnp.where(lead, 3, jnp.where(extra, 5, 4)))
+
+        @pl.when(lead)
+        def _():
+            copy_to(part_rows(psend, FAR), relay_p, 9, 23, paired).start()
+            copy_to(own_send, relay_l, 1, 24, paired).start()
+
+        @pl.when(aide)
+        def _():
+            landed(relay_p, 23)
+            copy_to(relay_p, relay_p, 10, 23, peer[FAR]).start()
+            landed(relay_l, 24)
+            copy_to(relay_l, relay_l, 11, 24, peer[FAR]).start()
+
+        @pl.when(led)
+        def _():
+            send_part(FAR)
+            send_list(FAR)
+
+        for o in (NEAR, SM, SP):
             send_list(o)
 
     pl.when(g != 0)(first_sends)
@@ -190,7 +220,7 @@
 
     if cf.shape[1] > stencil * nrow:
         cf[...] = jnp.zeros_like(cf)
-        sq[...] = jnp.zeros_like(sq)
+        sidx2[...] = jnp.zeros_like(sidx2)
     for k in range(4):
         for r in range(nrow):
             cols = cols_of(r)
@@ -216,7 +246,7 @@
         for t in range(erow):
             tan2[c * erow + t : c * erow + t + 1, :] = tan[c : c + 1, cols_of(t)]
     for r in range(nrow):
-        sq[pl.ds(r, stencil, stride=nrow), :] = sidx[:, cols_of(r)]
+        sidx2[pl.ds(r, stencil, stride=nrow), :] = sidx[:, cols_of(r)]
 
     def place(ref, at, f, b, r):
         hit = wide(own_list(f, b, r) >> 7, vrow) == rpart
@@ -230,9 +260,17 @@
     parts_left = lambda: left(psend.at[pl.ds(sent, 3 * sent)], 0)
     pl.when(g == G - 1)(parts_left)
 
-    @pl.when(seam)
+    def send_factor():
+        copy_to(cf, gcf, 2, 3, peer[FAR]).start()
+
+    pl.when(seam & led)(send_factor)
+
+    @pl.when(far_aide)
     def _():
-        copy_to(cf, gcf, 2, 3, peer[FAR]).start()
+        landed(relay_p, 23)
+        copy_to(relay_p, part_rows(got_p, FAR), 10, 0, paired).start()
+        landed(relay_l, 24)
+        copy_to(relay_l, got_send.at[FAR - 1], 11, 25, paired).start()
 
     landed(got_p.at[pl.ds(sent, 3 * sent)], 1)
     for f in range(2):
@@ -249,6 +287,23 @@
     got = nt_dot(spread3[...], onehot3[...])
     own_sum = own_sum + (got[:vrow] + got[vrow:])
 
+    def compose(x, y, parts):
+        lane = x & (LANES - 1)
+        row = x >> 7
+        for o in parts:
+            block = {FAR: far_block, NEAR: near_block, SM: 5, SP: 7}[o]
+            for h in range(2):
+                a, b = {FAR: (even, h), NEAR: (odd, h), SM: (h, 1), SP: (h, 0)}[o]
+                for r in range(nrow):
+                    line = got_send[o - 1, a, b : b + 1, cols_of(r)]
+                    line = jnp.broadcast_to(line + o * nrow * LANES, x.shape)
+                    y = jnp.where(row == (block + h) * nrow + r, lane_gather(line, lane), y)
+        return y
+
+    landed(got_send.at[pl.ds(NEAR - 1, 3)], 2)
+    for w in tiles:
+        sq[w, :] = compose(sidx2[w, :], sidx2[w, :], (NEAR, SM, SP))
+
     landed(part_rows(got_p, FAR), 0)
     half = len(lists) // 2
     for n, (f, b, r) in enumerate(lists[:half]):
@@ -277,32 +332,21 @@
             def _():
                 send_table(rnd, peer[FAR], FAR)
 
-    def compose(x):
-        lane = x & (LANES - 1)
-        row = x >> 7
-        y = x
-        for o in (FAR, NEAR, SM, SP):
-            block = {FAR: far_block, NEAR: near_block, SM: 5, SP: 7}[o]
-            for h in range(2):
-                a, b = {FAR: (even, h), NEAR: (odd, h), SM: (h, 1), SP: (h, 0)}[o]
-                for r in range(nrow):
-                    line = got_send[o - 1, a, b : b + 1, cols_of(r)]
-                    line = jnp.broadcast_to(line + o * nrow * LANES, x.shape)
-                    y = jnp.where(row == (block + h) * nrow + r, lane_gather(line, lane), y)
-        return y
-
-    def compose_all():
-        landed(got_send, 2)
+    def compose_far():
+        landed(got_send.at[FAR - 1], 25)
         for w in tiles:
-            sq[w, :] = compose(sq[w, :])
+            sq[w, :] = compose(sidx2[w, :], sq[w, :], (FAR,))
 
         @pl.when(seam)
         def _():
             copy_to(sq, gq, 3, 4, peer[FAR]).start()
 
+        pl.when(lead)(send_factor)
+
     def compose_heads():
         for i in range(erow // 8):
-            y = compose(head[i * 8 : i * 8 + 8, :])
+            x = head[i * 8 : i * 8 + 8, :]
+            y = compose(x, x, (FAR, NEAR, SM, SP))
             hq[i * 8 : i * 8 + 8, :] = y >> 7
             hl[i * 8 : i * 8 + 8, :] = y & (LANES - 1)
 
@@ -354,7 +398,6 @@
     def ghost_start(at):
         return tab[0, FAR * vrow + at : FAR * vrow + at + 8, :]
 
-    s_odd = lax.rem(s, 2)
     partner, across = SP - s_odd, SM + s_odd
     second, third = SM - s_odd, NEAR + 2 * s_odd
 
@@ -365,12 +408,13 @@
         either((partner, second, third, FAR), (partner, across, FAR, NEAR)),
         either((partner, second, FAR, third), (partner, across, FAR, NEAR)),
     )
-    fast_order = either((FAR, partner, second, third), (partner, across, FAR, NEAR))
+    late_order = either((partner, second, third, FAR), (partner, across, FAR, NEAR))
+    early_order = either((FAR, partner, second, third), (partner, across, FAR, NEAR))
 
     for rnd in range(0, SWEEPS, 2):
         send_round(rnd, True)
         if rnd == 0:
-            compose_all()
+            compose_far()
             compose_heads()
         add, accs = open_sweep(rnd, sq)
         add(OWN)
@@ -396,8 +440,7 @@
             add, accs = open_sweep(rnd + 1, sq)
         add(OWN)
 
-        @pl.when(seam)
-        def _():
+        def ghost_tables():
             if rnd == 0:
                 landed(gq, 4)
             ghost_add, ghost_accs = open_sweep(rnd, gq)
@@ -406,18 +449,36 @@
             table_here(rnd, FAR_NEAR, 3)
             for part in (NEAR, SM, SP):
                 ghost_add(part, GHOST_SLOT[part])
-            if rnd == 0:
-                landed(gcf, 3)
-            close_sweep(rnd, ghost_accs, gcf, ghost_start, FAR)
-
-        @pl.when(plain)
-        def _():
-            table_here(rnd + 1, partner)
-
-        for n, part in enumerate(fast_order):
-            if n:
-                table_here(rnd + 1, part)
-            add(part)
+            return ghost_accs
+
+        def ghost_begin():
+            for n, v in enumerate(sum(ghost_tables(), [])):
+                gacc[n * 8 : n * 8 + 8, :] = v
+
+        def ghost_end():
+            landed(gcf, 3)
+            held = [[gacc[n * 8 : n * 8 + 8, :] for n in range(4 * i, 4 * i + 4)] for i in range(len(tiles))]
+            close_sweep(rnd, held, gcf, ghost_start, FAR)
+
+        def ghost_whole():
+            close_sweep(rnd, ghost_tables(), gcf, ghost_start, FAR)
+
+        if not final:
+            pl.when(seam)(ghost_begin)
+            for n, part in enumerate(late_order):
+                if n < 3:
+                    table_here(rnd + 1, part)
+                else:
+                    pl.when(seam)(ghost_end)
+                    pl.when(plain)(lambda: table_here(rnd + 1, NEAR))
+                add(part)
+        else:
+            pl.when(seam)(ghost_whole)
+            pl.when(plain)(lambda: table_here(rnd + 1, partner))
+            for n, part in enumerate(early_order):
+                if n:
+                    table_here(rnd + 1, part)
+                add(part)
         if not final:
             close_sweep(rnd + 1, accs, cf, own_start, OWN)
 
@@ -436,6 +497,11 @@
     def _():
         left(cf, 2)
         left(sq, 3)
+
+    @pl.when(either_aide)
+    def _():
+        left(relay_p, 10)
+        left(relay_l, 11)
 
     for rnd in range(SWEEPS):
         counts = ((inner, 4), (feeds, 5), (seam, 6)) if rnd % 2 == 0 else ((plain, 4), (seam, 3))
@@ -454,7 +520,7 @@
     vrow = 4 * nrow
     stencil = stencil_index.shape[0]
     qrow = -(-stencil * nrow // 8) * 8
-    assert send_index.shape == (2, 2, nodes) and lax.axis_size("grp") % 2 == 0 and lax.axis_size("grp") > 4
+    assert send_index.shape == (2, 2, nodes) and lax.axis_size("grp") % 2 == 0 and lax.axis_size("grp") > 4 and lax.axis_size("sub") % 2 == 0
     coef = jnp.transpose(stencil_coef, (1, 0, 2))
     square = lambda x: x.reshape(erow, LANES)
     anyspace = pl.BlockSpec(memory_space=pl.ANY)
@@ -494,9 +560,13 @@
             vm((erow, LANES), I32),
             vm((qrow, LANES), I32),
             vm((qrow, LANES), I32),
+            vm((qrow, LANES), I32),
+            vm((4 * qrow, LANES), F32),
             vm((3 * erow, LANES), F32),
-            dma((10,)),
-            dma((5 + 9 * (SWEEPS // 2),)),
+            vm((2 * vrow, LANES), F32),
+            vm(send_index.shape, I32),
+            dma((12,)),
+            dma((8 + 9 * (SWEEPS // 2),)),
         ],
         compiler_params=pltpu.CompilerParams(collective_id=0, has_side_effects=True),
     )(

time: 24.4 us -> 24.4 us (level)
  no operation moved by 1% of the time
where the time goes in v5:
time: 24.4 us; the launch traced here: 24.2 us
  Pallas kernels  23.5 us (96%)
  local copies, waits for them, and re-layouts  0.6 us (2%)
    pallas_call x1, Pallas kernels, body(): pl.pallas_call(kernel, out_shape=vm((erow, LANES), F32), in_specs=[anyspa...  23.5 us
    unnamed x1, local copies, waits for them, and re-layouts  0.6 us

profile of v5, /device:TPU:1, one launch (start us, length us, event | category | flops | bytes accessed | tf_op | source)
XLA Modules:
  0.0 24.2 jit_solution(18185372477519888662)
XLA Ops:
  0.0 23.5 %shard_map.91 = f32[24,128]{1,0:T(8,128)S(1)} custom-call(f32[24,128]{1,0:T(8,128)} %bitcast.8, f32[3,3072]{1,0:T(4,128)} %tan_h.1, s32[24,128]{1,0:T(8,128)} %bitcast.9, s32[24,128]{1,0:T(8,128)} %bitcast.10, s32[14,512]{1,0:T(8,128)} %sidx_h.1, bf16[14,4,512]{2,1,0:T(4,128)(2,1)} %bitcast.7, f32[4,512]{1,0:T(4,128)} %marg_h.1, s32[2,2,512]{2,1,0:T(2,128)} %send_h.1, ...), custom_call_target="tpu_custom_call" | custom-call | tf_op jit(solution)/shard_map/pallas_call | solution.py:529
  23.6 0.6 %copy.11 = f32[3072]{0:T(1024)} copy(f32[3072]{0:T(1024)S(1)} %bitcast.6) | data formatting | bytes 24576

commit v6 on v5

--- a/solution.py
+++ b/solution.py
@@ -181,8 +181,9 @@
         c.wait()
     psend[0:sent] = scatter(spread_f, head, [base_of(far_block), base_of(far_block + 1)], 1, make=True)
 
+    extra = (g == 1) & (s_odd == 0)
+
     def first_sends():
-        extra = (g == 1) & (s_odd == 0)
         pl.semaphore_wait(barrier, jnp.where(lead, 3, jnp.where(extra, 5, 4)))
 
         @pl.when(lead)
@@ -205,14 +206,15 @@
         for o in (NEAR, SM, SP):
             send_list(o)
 
-    pl.when(g != 0)(first_sends)
+    late = (g == 0) | extra
+    pl.when(jnp.logical_not(late))(first_sends)
     rest = scatter(
         spread_r, head,
         [base_of(b) for b in (near_block, near_block + 1, 5, 6, 7, 8, 0)], 1,
     )
     psend[sent:] = rest[: 3 * sent]
     own_sum = rest[3 * sent :]
-    pl.when(g == 0)(first_sends)
+    pl.when(late)(first_sends)
     for o in (NEAR, SM, SP):
         send_part(o)
     for c in local[4:]:
@@ -406,7 +408,7 @@
 
     slow_order = (
         either((partner, second, third, FAR), (partner, across, FAR, NEAR)),
-        either((partner, second, FAR, third), (partner, across, FAR, NEAR)),
+        either((partner, second, third, FAR), (partner, across, NEAR, FAR)),
     )
     late_order = either((partner, second, third, FAR), (partner, across, FAR, NEAR))
     early_order = either((FAR, partner, second, third), (partner, across, FAR, NEAR))

time: 24.4 us -> 23.8 us (0.975)
  Pallas kernels: 23.5 us -> 23 us
    pallas_call x1, Pallas kernels: 23.5 us -> 23 us  [body(): pl.pallas_call(kernel, out_shape=vm((erow, LANES), F32), in_specs=[anyspa...]
where the time goes in v6:
time: 23.8 us; the launch traced here: 23.6 us
  Pallas kernels  23 us (97%)
  local copies, waits for them, and re-layouts  0.6 us (3%)
    pallas_call x1, Pallas kernels, body(): pl.pallas_call(kernel, out_shape=vm((erow, LANES), F32), in_specs=[anyspa...  23 us
    unnamed x1, local copies, waits for them, and re-layouts  0.6 us

profile of v6, /device:TPU:1, one launch (start us, length us, event | category | flops | bytes accessed | tf_op | source)
XLA Modules:
  0.0 23.6 jit_solution(984876426972203613)
XLA Ops:
  0.0 23.0 %shard_map.91 = f32[24,128]{1,0:T(8,128)S(1)} custom-call(f32[24,128]{1,0:T(8,128)} %bitcast.8, f32[3,3072]{1,0:T(4,128)} %tan_h.1, s32[24,128]{1,0:T(8,128)} %bitcast.9, s32[24,128]{1,0:T(8,128)} %bitcast.10, s32[14,512]{1,0:T(8,128)} %sidx_h.1, bf16[14,4,512]{2,1,0:T(4,128)(2,1)} %bitcast.7, f32[4,512]{1,0:T(4,128)} %marg_h.1, s32[2,2,512]{2,1,0:T(2,128)} %send_h.1, ...), custom_call_target="tpu_custom_call" | custom-call | tf_op jit(solution)/shard_map/pallas_call | solution.py:531
  23.0 0.6 %copy.11 = f32[3072]{0:T(1024)} copy(f32[3072]{0:T(1024)S(1)} %bitcast.6) | data formatting | bytes 24576

commit v7 on v6

--- a/solution.py
+++ b/solution.py
@@ -75,18 +75,18 @@
     tiles = [slice(i * 8, i * 8 + 8) for i in range(sq.shape[0] // 8)]
 
     barrier = pltpu.get_barrier_semaphore()
-    for o in (NEAR, SM, SP):
-        pl.semaphore_signal(barrier, inc=1, device_id=peer[o], device_id_type=MESH)
-
     skip = (g == G - 1) & (s_odd == 0)
     greeted = (jnp.where(skip, lax.rem(g + 2, G), gf), s)
-    pl.semaphore_signal(barrier, inc=1, device_id=greeted, device_id_type=MESH)
+    for who in (greeted, peer[NEAR], peer[SM], peer[SP]):
+        pl.semaphore_signal(barrier, inc=1, device_id=who, device_id_type=MESH)
 
     pairs = (
         (head_h, head, 0), (res_h, res, 4), (tan_h, tan, 5), (send_h, own_send, 1), (tail_h, tail, 2),
-        (coef_h, coef, 3), (marg_h, marg, 6), (sidx_h, sidx, 7), (scale_h, scale, 8),
+        (coef_h, coef, 3), (marg_h, marg, 14), (sidx_h, sidx, 15), (scale_h, scale, 16),
     )
-    local = [pltpu.make_async_copy(src, dst, send_sem.at[i]) for src, dst, i in pairs]
+    local = [
+        pltpu.make_async_copy(src, dst, send_sem.at[i] if i < 14 else recv_sem.at[i]) for src, dst, i in pairs
+    ]
     for c in local:
         c.start()
 
@@ -107,10 +107,10 @@
 
     def send_part(o):
         far = o == FAR
-        copy_to(part_rows(psend, o), part_rows(got_p, back[o]), 9 if far else 0, 0 if far else 1, peer[o]).start()
+        copy_to(part_rows(psend, o), part_rows(got_p, back[o]), 5 if far else 0, 0 if far else 1, peer[o]).start()
 
     def send_list(o):
-        copy_to(own_send, got_send.at[back[o] - 1], 1, 25 if o == FAR else 2, peer[o]).start()
+        copy_to(own_send, got_send.at[back[o] - 1], 1, 23 if o == FAR else 2, peer[o]).start()
 
     def slot_rows(rnd, slot):
         return tab.at[rnd, pl.ds(slot * vrow, vrow)]
@@ -120,7 +120,7 @@
         return 5 + 9 * (rnd // 2) + slot - 1 + FAR_NEAR * (rnd % 2)
 
     def send_table(rnd, who, slot):
-        copy_to(slot_rows(rnd, OWN), slot_rows(rnd, slot), 4 + rnd, table_sem(rnd, slot), who).start()
+        copy_to(slot_rows(rnd, OWN), slot_rows(rnd, slot), 4, table_sem(rnd, slot), who).start()
 
     def table_here(rnd, first, count=1):
         landed(tab.at[rnd, pl.ds(first * vrow, count * vrow)], table_sem(rnd, first))
@@ -188,15 +188,15 @@
 
         @pl.when(lead)
         def _():
-            copy_to(part_rows(psend, FAR), relay_p, 9, 23, paired).start()
-            copy_to(own_send, relay_l, 1, 24, paired).start()
+            copy_to(part_rows(psend, FAR), relay_p, 5, 10, paired).start()
+            copy_to(own_send, relay_l, 1, 19, paired).start()
 
         @pl.when(aide)
         def _():
-            landed(relay_p, 23)
-            copy_to(relay_p, relay_p, 10, 23, peer[FAR]).start()
-            landed(relay_l, 24)
-            copy_to(relay_l, relay_l, 11, 24, peer[FAR]).start()
+            landed(relay_p, 10)
+            copy_to(relay_p, relay_p, 6, 10, peer[FAR]).start()
+            landed(relay_l, 19)
+            copy_to(relay_l, relay_l, 7, 19, peer[FAR]).start()
 
         @pl.when(led)
         def _():
@@ -269,10 +269,27 @@
 
     @pl.when(far_aide)
     def _():
-        landed(relay_p, 23)
-        copy_to(relay_p, part_rows(got_p, FAR), 10, 0, paired).start()
-        landed(relay_l, 24)
-        copy_to(relay_l, got_send.at[FAR - 1], 11, 25, paired).start()
+        landed(relay_p, 10)
+        copy_to(relay_p, part_rows(got_p, FAR), 6, 0, paired).start()
+        landed(relay_l, 19)
+        copy_to(relay_l, got_send.at[FAR - 1], 7, 23, paired).start()
+
+    def compose(x, y, parts):
+        lane = x & (LANES - 1)
+        row = x >> 7
+        for o in parts:
+            block = {FAR: far_block, NEAR: near_block, SM: 5, SP: 7}[o]
+            for h in range(2):
+                a, b = {FAR: (even, h), NEAR: (odd, h), SM: (h, 1), SP: (h, 0)}[o]
+                for r in range(nrow):
+                    line = got_send[o - 1, a, b : b + 1, cols_of(r)]
+                    line = jnp.broadcast_to(line + o * nrow * LANES, x.shape)
+                    y = jnp.where(row == (block + h) * nrow + r, lane_gather(line, lane), y)
+        return y
+
+    landed(got_send.at[pl.ds(NEAR - 1, 3)], 2)
+    for w in tiles:
+        sq[w, :] = compose(sidx2[w, :], sidx2[w, :], (NEAR, SM, SP))
 
     landed(got_p.at[pl.ds(sent, 3 * sent)], 1)
     for f in range(2):
@@ -289,23 +306,6 @@
     got = nt_dot(spread3[...], onehot3[...])
     own_sum = own_sum + (got[:vrow] + got[vrow:])
 
-    def compose(x, y, parts):
-        lane = x & (LANES - 1)
-        row = x >> 7
-        for o in parts:
-            block = {FAR: far_block, NEAR: near_block, SM: 5, SP: 7}[o]
-            for h in range(2):
-                a, b = {FAR: (even, h), NEAR: (odd, h), SM: (h, 1), SP: (h, 0)}[o]
-                for r in range(nrow):
-                    line = got_send[o - 1, a, b : b + 1, cols_of(r)]
-                    line = jnp.broadcast_to(line + o * nrow * LANES, x.shape)
-                    y = jnp.where(row == (block + h) * nrow + r, lane_gather(line, lane), y)
-        return y
-
-    landed(got_send.at[pl.ds(NEAR - 1, 3)], 2)
-    for w in tiles:
-        sq[w, :] = compose(sidx2[w, :], sidx2[w, :], (NEAR, SM, SP))
-
     landed(part_rows(got_p, FAR), 0)
     half = len(lists) // 2
     for n, (f, b, r) in enumerate(lists[:half]):
@@ -335,7 +335,7 @@
                 send_table(rnd, peer[FAR], FAR)
 
     def compose_far():
-        landed(got_send.at[FAR - 1], 25)
+        landed(got_send.at[FAR - 1], 23)
         for w in tiles:
             sq[w, :] = compose(sidx2[w, :], sq[w, :], (FAR,))
 
@@ -492,7 +492,7 @@
         out_ref[w, :] = scale[w, :] * res[w, :] + ((hacc[i][0] - tacc[i][0]) + 0.5 * mixed)
 
     pl.when(g != G - 1)(parts_left)
-    left(part_rows(psend, FAR), 9)
+    left(part_rows(psend, FAR), 5)
     left(got_send, 1)
 
     @pl.when(seam)
@@ -502,13 +502,11 @@
 
     @pl.when(either_aide)
     def _():
-        left(relay_p, 10)
-        left(relay_l, 11)
-
-    for rnd in range(SWEEPS):
-        counts = ((inner, 4), (feeds, 5), (seam, 6)) if rnd % 2 == 0 else ((plain, 4), (seam, 3))
-        for which, n in counts:
-            pl.when(which)(lambda n=n: left(tab.at[rnd, pl.ds(0, n * vrow)], 4 + rnd))
+        left(relay_p, 6)
+        left(relay_l, 7)
+
+    pl.when(inner)(lambda: left(tab.at[pl.ds(0, 2)], 4))
+    pl.when(jnp.logical_not(inner))(lambda: left(tab.at[pl.ds(0, 3), pl.ds(0, 6 * vrow)], 4))
 
 
 def body(
@@ -567,8 +565,8 @@
             vm((3 * erow, LANES), F32),
             vm((2 * vrow, LANES), F32),
             vm(send_index.shape, I32),
-            dma((12,)),
-            dma((8 + 9 * (SWEEPS // 2),)),
+            dma((8,)),
+            dma((6 + 9 * (SWEEPS // 2),)),
         ],
         compiler_params=pltpu.CompilerParams(collective_id=0, has_side_effects=True),
     )(

time: 23.8 us -> 23.7 us (level)
  no operation moved by 1% of the time
where the time goes in v7:
time: 23.7 us; the launch traced here: 23.5 us
  Pallas kernels  22.9 us (97%)
  local copies, waits for them, and re-layouts  0.6 us (3%)
    pallas_call x1, Pallas kernels, body(): pl.pallas_call(kernel, out_shape=vm((erow, LANES), F32), in_specs=[anyspa...  22.9 us
    unnamed x1, local copies, waits for them, and re-layouts  0.6 us

profile of v7, /device:TPU:1, one launch (start us, length us, event | category | flops | bytes accessed | tf_op | source)
XLA Modules:
  0.0 23.5 jit_solution(4885702722443188777)
XLA Ops:
  0.0 22.9 %shard_map.91 = f32[24,128]{1,0:T(8,128)S(1)} custom-call(f32[24,128]{1,0:T(8,128)} %bitcast.8, f32[3,3072]{1,0:T(4,128)} %tan_h.1, s32[24,128]{1,0:T(8,128)} %bitcast.9, s32[24,128]{1,0:T(8,128)} %bitcast.10, s32[14,512]{1,0:T(8,128)} %sidx_h.1, bf16[14,4,512]{2,1,0:T(4,128)(2,1)} %bitcast.7, f32[4,512]{1,0:T(4,128)} %marg_h.1, s32[2,2,512]{2,1,0:T(2,128)} %send_h.1, ...), custom_call_target="tpu_custom_call" | custom-call | tf_op jit(solution)/shard_map/pallas_call | solution.py:529
  22.9 0.6 %copy.11 = f32[3072]{0:T(1024)} copy(f32[3072]{0:T(1024)S(1)} %bitcast.6) | data formatting | bytes 24576
